TPU v7x, 128 devices: a whole 4x4x4 slice. The times are simulated.
128 devices in a mesh: lat: 8 (over x, core), lon: 16 (over y, z).
Axes of the slice: x: 4, y: 4, z: 4, core: 2. Of those that a mesh axis runs over, the one named last changes fastest.
Arguments:
- zonal_wind: float32 [16, 64, 4096], P(None, 'lat', 'lon'), may hold values from -0.45 to 0.45
- merid_wind: float32 [16, 64, 4096], P(None, 'lat', 'lon'), may hold values from -0.45 to 0.45
- operator_rows: float32 [8, 64], replicated, may hold values from -1.5 to 1.5
- innovation: float32 [524288], P(('lat', 'lon')), may hold values from -6 to 6
- error_weight: float32 [524288], P(('lat', 'lon')), may hold values from 0.25 to 4
- interp_weight: float32 [4, 524288], P(None, ('lat', 'lon')), may hold values from 0.05 to 1
- obs_slot: int32 [4, 524288], P(None, ('lat', 'lon')), may hold values from 0 to 2047
- block_count: int32 [4096], P(('lat', 'lon')), may hold values from 1 to 128
- block_type: int32 [4096], P(('lat', 'lon')), may hold values from 0 to 7
- block_window: int32 [4096], P(('lat', 'lon')), may hold values from 0 to 2
- send_cols: int32 [128, 2048], P(('lat', 'lon')), may hold values from 0 to 2047
Outputs:
- increment: float32 [4, 16, 64, 4096], P(None, None, 'lat', 'lon')
- residual: float32 [4, 16, 64, 4096], P(None, None, 'lat', 'lon')
Inputs may be any that keep to these rules, and one draw needn't show every extreme that they name: `obs_slot`: an index into the 2048 slots that the observation's own device receives: slot s * 16 + q comes from device s. `send_cols`: entry r * 16 + q of device s's row is a local cell of device s, row-major over 8 x 256, sent to slot q of device r. `block_count`: rows of a block at or past its count are padding and observe nothing.
All inputs are finite; a program needn't handle non-finite values.
Results may differ from a plain program's by a relative error of at most 0.00025.
Values sent between devices are 32-bit elements; how exact they have to be, the bound alone decides.
A program may use at most 128 MiB of HBM per device.

v0:
```python
import jax
import jax.numpy as jnp
from jax import lax
from jax.sharding import Mesh
from jax.sharding import PartitionSpec as P

TYPES = 8
WIN = 3
STEP_WIN = 2
ITERS = 2
BLOCK_ROWS = 128
LON = ("lon_0", "lon_1")
LAT = ("lat_0", "lat_1")
LAT_LON = ("lat_0", "lat_1", "lon_0", "lon_1")


HIGH = lax.Precision.HIGHEST


def padded(cells, sides, width, closed):
    for axis, dim in sides:
        count = lax.axis_size(axis)
        ends = count if closed else count - 1
        head = lax.slice_in_dim(cells, 0, width, axis=dim)
        tail = lax.slice_in_dim(cells, cells.shape[dim] - width, cells.shape[dim], axis=dim)
        cells = jnp.concatenate(
            [
                lax.ppermute(tail, axis, [(i, (i + 1) % count) for i in range(ends)]),
                cells,
                lax.ppermute(head, axis, [((i + 1) % count, i) for i in range(ends)]),
            ],
            axis=dim,
        )
    return cells


def by_axis(array, axes):
    for axis in axes:
        array = lax.psum(array, axis)
    return array


def over_pieces(array, axis):
    blocks = lax.all_gather(array, axis)
    return blocks.sum(axis=0)


def extend(field, width):
    widened = padded(field, ((LON, 3),), width, True)
    return padded(widened, ((LAT, 2),), width, False)


def squares(residual):
    return by_axis(jnp.sum(residual * residual), LAT_LON)


def advance(field, margin, adjoint, winds, valid_rows):
    keep_rate, from_west, from_east, from_south, from_north = winds
    lat_out = keep_rate.shape[1] - 4 + 2 * margin - 2
    lon_out = keep_rate.shape[2] - 4 + 2 * margin - 2
    offset = 3 - margin

    def wind(array, shift_lat, shift_lon):
        return array[
            :,
            offset + shift_lat : offset + shift_lat + lat_out,
            offset + shift_lon : offset + shift_lon + lon_out,
        ]

    def cur(shift_lat, shift_lon):
        return field[
            :, :, 1 + shift_lat : 1 + shift_lat + lat_out, 1 + shift_lon : 1 + shift_lon + lon_out
        ]

    if adjoint:
        result = (
            wind(keep_rate, 0, 0) * cur(0, 0)
            + wind(from_west, 0, 1) * cur(0, 1)
            - wind(from_east, 0, -1) * cur(0, -1)
            + wind(from_south, 1, 0) * cur(1, 0)
            - wind(from_north, -1, 0) * cur(-1, 0)
        )
    else:
        result = (
            wind(keep_rate, 0, 0) * cur(0, 0)
            + wind(from_west, 0, 0) * cur(0, -1)
            - wind(from_east, 0, 0) * cur(0, 1)
            + wind(from_south, 0, 0) * cur(-1, 0)
            - wind(from_north, 0, 0) * cur(1, 0)
        )
    mask = valid_rows[offset : offset + lat_out][:, None]
    return result * mask


def shards(
    zonal_wind,
    merid_wind,
    operator_rows,
    innovation,
    error_weight,
    interp_weight,
    obs_slot,
    block_count,
    block_type,
    block_window,
    send_cols,
):
    levels, lat_cells, lon_cells = zonal_wind.shape
    channels = operator_rows.shape[1]
    layers = channels // levels
    cells = lat_cells * lon_cells
    recv = send_cols.shape[1]
    blocks = block_count.shape[0]
    rows = innovation.shape[0]
    send_row = send_cols[0]
    total_rows = lax.axis_size(LAT) * lat_cells
    wind_rims = extend(jnp.stack([zonal_wind, merid_wind]), 2)
    keep_ext = 1.0 - jnp.abs(wind_rims[0]) - jnp.abs(wind_rims[1])
    winds = (
        keep_ext,
        jnp.maximum(wind_rims[0], 0.0),
        jnp.minimum(wind_rims[0], 0.0),
        jnp.maximum(wind_rims[1], 0.0),
        jnp.minimum(wind_rims[1], 0.0),
    )
    global_rows = lax.axis_index(LAT) * lat_cells - 2 + jnp.arange(lat_cells + 4, dtype=jnp.int32)
    valid_rows = ((global_rows >= 0) & (global_rows < total_rows)).astype(jnp.float32)
    live = (jnp.arange(BLOCK_ROWS, dtype=jnp.int32)[None, :] < block_count[:, None]).reshape(rows)
    weight_live = error_weight * live.astype(jnp.float32)
    row_type = jnp.broadcast_to(block_type[:, None], (blocks, BLOCK_ROWS)).reshape(rows)
    row_window = jnp.broadcast_to(block_window[:, None], (blocks, BLOCK_ROWS)).reshape(rows)
    flat_index = (row_window * TYPES + row_type)[None, :] * recv + obs_slot

    def run_steps(field, count, adjoint):
        remaining = count
        while remaining > 0:
            depth = min(2, remaining)
            extended = extend(field, depth)
            for section in range(depth):
                extended = advance(extended, depth - section, adjoint, winds, valid_rows)
            field = extended
            remaining = remaining - depth
        return field

    def forward_model(field):
        states = [field]
        for _ in range(WIN - 1):
            field = run_steps(field, STEP_WIN, False)
            states.append(field)
        return states

    def adjoint_model(weighted):
        terms = (interp_weight * weighted[None, :]).reshape(-1)
        summed = jax.ops.segment_sum(
            terms, flat_index.reshape(-1), num_segments=WIN * TYPES * recv
        ).reshape(WIN, TYPES, recv)
        typed_back = lax.all_to_all(
            summed.reshape(WIN * TYPES, recv), LAT_LON, split_axis=1, concat_axis=1, tiled=True
        ).reshape(WIN, TYPES, recv)
        returned = jnp.einsum("tc,wts->wcs", operator_rows, typed_back, precision=HIGH)
        forcing = [
            jnp.zeros((channels, cells), jnp.float32)
            .at[:, send_row]
            .add(returned[window])
            .reshape(layers, levels, lat_cells, lon_cells)
            for window in range(WIN)
        ]
        field = forcing[WIN - 1]
        for window in range(WIN - 2, -1, -1):
            field = run_steps(field, STEP_WIN, True)
            field = field + forcing[window]
        return field

    right = adjoint_model(weight_live * innovation)
    increment = jnp.zeros_like(right)
    residual = right
    direction = right
    norm_now = squares(residual)
    for _ in range(ITERS):
        observe_states = forward_model(direction)
        picked = jnp.stack(
            [jnp.take(state.reshape(channels, cells), send_row, axis=1) for state in observe_states]
        )
        typed = jnp.einsum("tc,wcs->wts", operator_rows, picked, precision=HIGH)
        images = lax.all_to_all(
            typed.reshape(WIN * TYPES, recv), LAT_LON, split_axis=1, concat_axis=1, tiled=True
        )
        values = images.reshape(-1)[flat_index]
        image = direction + adjoint_model(weight_live * jnp.sum(interp_weight * values, axis=0))
        alpha = norm_now / over_pieces(jnp.sum(direction * image), LAT_LON)
        increment = increment + alpha * direction
        residual = residual - alpha * image
        norm_next = squares(residual)
        direction = residual + norm_next / norm_now * direction
        norm_now = norm_next
    return (increment, residual)


def solution(mesh):
    finer = Mesh(mesh.devices.reshape(4, 2, 4, 4), ("lat_0", "lat_1", "lon_0", "lon_1"))
    in_specs = (
        P(None, LAT, LON),
        P(None, LAT, LON),
        P(),
        P(LAT_LON),
        P(LAT_LON),
        P(None, LAT_LON),
        P(None, LAT_LON),
        P(LAT_LON),
        P(LAT_LON),
        P(LAT_LON),
        P(LAT_LON, None),
    )
    out_specs = (P(None, None, LAT, LON), P(None, None, LAT, LON))
    return jax.shard_map(
        shards, mesh=finer, in_specs=in_specs, out_specs=out_specs, check_vma=False
    )
```

profile of v0, /device:TPU:1, one launch (start us, length us, event | category | flops | bytes accessed | tf_op | source)
XLA Modules:
  0.0 1311.2 jit_solution(10959441893060576444)
XLA Ops:
  4.6 86.5 %scatter_custom_fusion = f32[49152]{0:T(1024)S(1)} fusion(s32[16384]{0:T(1024)S(1)} %bitcast.258, f32[16384]{0:T(1024)S(1)} %bitcast.262, f32[]{:T(128)} %constant.22.clone.1), kind=kCustom, calls=%fused_computation.403 | custom fusion | flops 16384 | bytes 196612 | tf_op jit(solution)/shard_map/scatter-add | solution.py:154
  94.0 11.9 all-to-all-start
  144.7 12.8 scatter_custom_fusion.1
  182.2 12.8 scatter_custom_fusion.2
  205.2 5.4 collective-permute-start.9
  216.8 5.9 collective-permute-start.10
  226.9 13.2 %scatter_custom_fusion.3 = f32[64,2048]{0,1:T(8,128)} fusion(s32[2048]{0:T(1024)} %bitcast.266, f32[2048,64]{1,0:T(8,128)} %copy.85, f32[]{:T(128)} %constant.22.clone.1), kind=kCustom, calls=%fused_computation.349 | custom fusion | flops 131072 | bytes 524800 | tf_op jit(solution)/shard_map/scatter-add | solution.py:164
  259.5 5.6 collective-permute-start.14
  276.7 4.8 collective-permute-start.17
  286.6 5.4 collective-permute-start.18
  297.0 7.6 gather_fusion.2
  309.4 7.6 gather_fusion.3
  328.3 7.6 gather_fusion.4
  345.8 7.9 all-to-all-start.1
  353.7 10.4 all-to-all-done.1
  370.1 90.5 %gather_fusion = f32[16384]{0:T(1024)S(1)} fusion(f32[49152]{0:T(1024)S(1)} %reshape.198, s32[16384]{0:T(1024)S(1)} %broadcast_clamp_fusion), kind=kCustom, calls=%fused_computation.6 | custom fusion | bytes 196608 | tf_op jit(solution)/shard_map/gather | solution.py:188
  460.8 86.7 %scatter_custom_fusion.4 = f32[49152]{0:T(1024)S(1)} fusion(s32[16384]{0:T(1024)} %bitcast.259, f32[16384]{0:T(1024)S(1)} %bitcast.263, f32[]{:T(128)} %constant.22.clone.1), kind=kCustom, calls=%fused_computation.401 | custom fusion | flops 16384 | bytes 197120 | tf_op jit(solution)/shard_map/scatter-add | solution.py:154
  552.0 15.3 %all_to_all.45 = f32[128,1,384]{2,1,0:T(1,128)S(1)} all-to-all(f32[128,1,384]{2,1,0:T(1,128)S(1)} %reshape.431), channel_id=1, replica_groups=mesh['lat_0'=4,'lat_1'=2,'lon_0'=4,'lon_1'=4] {'lat_0','lat_1','lon_0','..., dimensions={0} | all-to-all | bytes 393216 | tf_op jit(solution)/shard_map/all_to_all | solution.py:157
  577.6 12.1 scatter_custom_fusion.5
  597.0 5.7 collective-permute-done.20
  612.1 12.9 scatter_custom_fusion.6
  635.4 4.8 collective-permute-start.25
  640.3 6.2 collective-permute-done.24
  655.9 12.8 scatter_custom_fusion.7
  679.3 8.5 psum.56
  687.8 5.8 psum.57
  693.6 6.7 psum.58
  701.0 65.9 %all-reduce = f32[128]{0:T(128)S(1)} all-reduce(f32[128]{0:T(128)S(1)} %dynamic-update-slice), channel_id=1, replica_groups=mesh['lat_0'=4,'lat_1'=2,'lon_0'=4,'lon_1'=4] {'lat_0','lat_1','lon_0','..., use_global_device_ids=true, to_apply=%add | all-reduce | flops 128 | bytes 1024
  766.9 8.8 psum.59
  778.4 7.3 psum.60
  785.7 7.4 psum.61
  793.1 7.7 psum.62
  800.8 7.1 psum.63
  818.7 8.3 collective-permute-start.30
  838.5 5.1 collective-permute-start.33
  857.9 7.6 gather_fusion.5
  870.3 7.6 gather_fusion.6
  889.3 7.6 gather_fusion.7
  906.8 18.6 %all_to_all.46 = f32[128,1,384]{2,1,0:T(1,128)S(1)} all-to-all(f32[128,1,384]{2,1,0:T(1,128)} %reshape.433), channel_id=1, replica_groups=mesh['lat_0'=4,'lat_1'=2,'lon_0'=4,'lon_1'=4] {'lat_0','lat_1','lon_0','..., dimensions={0} | all-to-all | bytes 393216 | tf_op jit(solution)/shard_map/all_to_all | solution.py:185
  932.9 90.5 %gather_fusion.1 = f32[16384]{0:T(1024)S(1)} fusion(f32[49152]{0:T(1024)S(1)} %reshape.207, s32[16384]{0:T(1024)S(1)} %copy-done.120), kind=kCustom, calls=%fused_computation.7 | custom fusion | bytes 196608 | tf_op jit(solution)/shard_map/gather | solution.py:188
  1023.7 86.7 %scatter_custom_fusion.8 = f32[49152]{0:T(1024)S(1)} fusion(s32[16384]{0:T(1024)} %bitcast.260, f32[16384]{0:T(1024)S(1)} %bitcast.261, f32[]{:T(128)} %constant.22.clone.1), kind=kCustom, calls=%fused_computation.399 | custom fusion | flops 16384 | bytes 197120 | tf_op jit(solution)/shard_map/scatter-add | solution.py:154
  1115.5 15.2 %all_to_all.47 = f32[128,1,384]{2,1,0:T(1,128)S(1)} all-to-all(f32[128,1,384]{2,1,0:T(1,128)} %reshape.435), channel_id=1, replica_groups=mesh['lat_0'=4,'lat_1'=2,'lon_0'=4,'lon_1'=4] {'lat_0','lat_1','lon_0','..., dimensions={0} | all-to-all | bytes 393216 | tf_op jit(solution)/shard_map/all_to_all | solution.py:157
  1142.7 12.1 scatter_custom_fusion.9
  1162.2 5.7 collective-permute-done.36
  1176.2 12.3 scatter_custom_fusion.10
  1202.7 6.2 collective-permute-done.40
  1217.6 12.8 scatter_custom_fusion.11
  1242.0 65.9 %all-reduce.1 = f32[128]{0:T(128)S(1)} all-reduce(f32[128]{0:T(128)S(1)} %dynamic-update-slice.1), channel_id=1, replica_groups=mesh['lat_0'=4,'lat_1'=2,'lon_0'=4,'lon_1'=4] {'lat_0','lat_1','lon_0','..., use_global_device_ids=true, to_apply=%add.1 | all-reduce | flops 128 | bytes 1024
  (540 shorter events, 363.5 us)
Async XLA Ops:
  94.0 36.6 %all-to-all-start = ((f32[128,1,384]{2,1,0:T(1,128)}), f32[128,1,384]{2,1,0:T(1,128)}, u32[]{:S(2)}, u32[]{:S(2)}) async-start(f32[128,1,384]{2,1,0:T(1,128)} %reshape.427), calls=%async_computation | async-start | bytes 393216 | tf_op jit(solution)/shard_map/all_to_all | solution.py:157
  106.1 10.9 collective-permute-start
  107.7 9.4 collective-permute-start.1
  117.4 5.8 collective-permute-start.2
  120.9 5.9 collective-permute-start.3
  130.6 543.5 %copy-start.1 = (f32[16,10,258]{2,1,0:T(8,128)}, f32[16,10,258]{2,1,0:T(8,128)S(1)}, u32[]{:S(2)}) copy-start(f32[16,10,258]{2,1,0:T(8,128)S(1)} %get-tuple-element.79) | copy-start | bytes 495364
  161.3 9.2 collective-permute-start.4
  161.4 9.1 collective-permute-start.5
  167.4 670.2 %copy-start.12 = (f32[16,8,256]{2,1,0:T(8,128)}, f32[16,8,256]{2,1,0:T(8,128)S(1)}, u32[]{:S(2)}) copy-start(f32[16,8,256]{2,1,0:T(8,128)S(1)} %slice.844) | copy-start | bytes 393220
  171.9 26.7 %collective-permute-start.6 = (f32[4,16,2,260]{3,2,1,0:T(2,128)}, f32[4,16,2,260]{3,2,1,0:T(2,128)}, u32[]{:S(2)}, u32[]{:S(2)}) collective-permute-start(f32[4,16,2,260]{3,2,1,0:T(2,128)} %get-tuple-element.36), channel_id=1, source_target_pairs={{0,16},{16,32},{32,48},{48,64},{64,80},{80,96},{96,112},{1,17},{17... | collective-permute-start | bytes 399368 | tf_op jit(solution)/shard_map/ppermute | solution.py:28
  176.7 21.9 %collective-permute-start.7 = (f32[4,16,2,260]{3,2,1,0:T(2,128)}, f32[4,16,2,260]{3,2,1,0:T(2,128)}, u32[]{:S(2)}, u32[]{:S(2)}) collective-permute-start(f32[4,16,2,260]{3,2,1,0:T(2,128)} %get-tuple-element.35), channel_id=1, source_target_pairs={{16,0},{32,16},{48,32},{64,48},{80,64},{96,80},{112,96},{17,1},{33... | collective-permute-start | bytes 399368 | tf_op jit(solution)/shard_map/ppermute | solution.py:30
  205.2 9.5 collective-permute-start.8
  205.2 9.5 collective-permute-start.9
  216.8 26.9 %collective-permute-start.10 = (f32[4,16,2,260]{3,2,1,0:T(2,128)}, f32[4,16,2,260]{3,2,1,0:T(2,128)}, u32[]{:S(2)}, u32[]{:S(2)}) collective-permute-start(f32[4,16,2,260]{3,2,1,0:T(2,128)} %get-tuple-element.34), channel_id=1, source_target_pairs={{0,16},{16,32},{32,48},{48,64},{64,80},{80,96},{96,112},{1,17},{17... | collective-permute-start | bytes 399368 | tf_op jit(solution)/shard_map/ppermute | solution.py:28
  222.6 21.1 %collective-permute-start.11 = (f32[4,16,2,260]{3,2,1,0:T(2,128)}, f32[4,16,2,260]{3,2,1,0:T(2,128)}, u32[]{:S(2)}, u32[]{:S(2)}) collective-permute-start(f32[4,16,2,260]{3,2,1,0:T(2,128)} %get-tuple-element.33), channel_id=1, source_target_pairs={{16,0},{32,16},{48,32},{64,48},{80,64},{96,80},{112,96},{17,1},{33... | collective-permute-start | bytes 399368 | tf_op jit(solution)/shard_map/ppermute | solution.py:30
  250.3 8.6 collective-permute-start.12
  250.4 8.5 collective-permute-start.13
  259.5 8.2 collective-permute-start.14
  265.2 7.0 collective-permute-start.15
  276.6 8.6 collective-permute-start.16
  276.7 8.5 collective-permute-start.17
  286.6 32.9 %collective-permute-start.18 = (f32[4,16,2,260]{3,2,1,0:T(2,128)}, f32[4,16,2,260]{3,2,1,0:T(2,128)}, u32[]{:S(2)}, u32[]{:S(2)}) collective-permute-start(f32[4,16,2,260]{3,2,1,0:T(2,128)} %get-tuple-element.29), channel_id=1, source_target_pairs={{0,16},{16,32},{32,48},{48,64},{64,80},{80,96},{96,112},{1,17},{17... | collective-permute-start | bytes 399368 | tf_op jit(solution)/shard_map/ppermute | solution.py:28
  292.0 27.5 %collective-permute-start.19 = (f32[4,16,2,260]{3,2,1,0:T(2,128)}, f32[4,16,2,260]{3,2,1,0:T(2,128)}, u32[]{:S(2)}, u32[]{:S(2)}) collective-permute-start(f32[4,16,2,260]{3,2,1,0:T(2,128)} %get-tuple-element.30), channel_id=1, source_target_pairs={{16,0},{32,16},{48,32},{64,48},{80,64},{96,80},{112,96},{17,1},{33... | collective-permute-start | bytes 399368 | tf_op jit(solution)/shard_map/ppermute | solution.py:30
  345.8 18.3 %all-to-all-start.1 = ((f32[128,1,384]{2,1,0:T(1,128)}), f32[128,1,384]{2,1,0:T(1,128)S(1)}, u32[]{:S(2)}, u32[]{:S(2)}) async-start(f32[128,1,384]{2,1,0:T(1,128)} %reshape.429), calls=%async_computation.1 | async-start | bytes 393216 | tf_op jit(solution)/shard_map/all_to_all | solution.py:185
  592.2 10.6 collective-permute-start.20
  592.8 10.0 collective-permute-start.21
  604.1 24.4 %collective-permute-start.22 = (f32[4,16,2,260]{3,2,1,0:T(2,128)}, f32[4,16,2,260]{3,2,1,0:T(2,128)}, u32[]{:S(2)}, u32[]{:S(2)}) collective-permute-start(f32[4,16,2,260]{3,2,1,0:T(2,128)} %get-tuple-element.28), channel_id=1, source_target_pairs={{0,16},{16,32},{32,48},{48,64},{64,80},{80,96},{96,112},{1,17},{17... | collective-permute-start | bytes 399368 | tf_op jit(solution)/shard_map/ppermute | solution.py:28
  607.8 20.8 %collective-permute-start.23 = (f32[4,16,2,260]{3,2,1,0:T(2,128)}, f32[4,16,2,260]{3,2,1,0:T(2,128)}, u32[]{:S(2)}, u32[]{:S(2)}) collective-permute-start(f32[4,16,2,260]{3,2,1,0:T(2,128)} %get-tuple-element.27), channel_id=1, source_target_pairs={{16,0},{32,16},{48,32},{64,48},{80,64},{96,80},{112,96},{17,1},{33... | collective-permute-start | bytes 399368 | tf_op jit(solution)/shard_map/ppermute | solution.py:30
  635.4 11.1 collective-permute-start.24
  635.4 11.0 collective-permute-start.25
  648.5 23.7 %collective-permute-start.26 = (f32[4,16,2,260]{3,2,1,0:T(2,128)}, f32[4,16,2,260]{3,2,1,0:T(2,128)}, u32[]{:S(2)}, u32[]{:S(2)}) collective-permute-start(f32[4,16,2,260]{3,2,1,0:T(2,128)} %get-tuple-element.26), channel_id=1, source_target_pairs={{0,16},{16,32},{32,48},{48,64},{64,80},{80,96},{96,112},{1,17},{17... | collective-permute-start | bytes 399368 | tf_op jit(solution)/shard_map/ppermute | solution.py:28
  651.4 20.8 %collective-permute-start.27 = (f32[4,16,2,260]{3,2,1,0:T(2,128)}, f32[4,16,2,260]{3,2,1,0:T(2,128)}, u32[]{:S(2)}, u32[]{:S(2)}) collective-permute-start(f32[4,16,2,260]{3,2,1,0:T(2,128)} %get-tuple-element.25), channel_id=1, source_target_pairs={{16,0},{32,16},{48,32},{64,48},{80,64},{96,80},{112,96},{17,1},{33... | collective-permute-start | bytes 399368 | tf_op jit(solution)/shard_map/ppermute | solution.py:30
  809.4 8.6 collective-permute-start.28
  810.6 7.5 collective-permute-start.29
  818.7 10.9 collective-permute-start.30
  827.0 7.0 collective-permute-start.31
  838.4 8.9 collective-permute-start.32
  838.5 8.8 collective-permute-start.33
  848.7 31.7 %collective-permute-start.34 = (f32[4,16,2,260]{3,2,1,0:T(2,128)}, f32[4,16,2,260]{3,2,1,0:T(2,128)}, u32[]{:S(2)}, u32[]{:S(2)}) collective-permute-start(f32[4,16,2,260]{3,2,1,0:T(2,128)} %get-tuple-element.21), channel_id=1, source_target_pairs={{0,16},{16,32},{32,48},{48,64},{64,80},{80,96},{96,112},{1,17},{17... | collective-permute-start | bytes 399368 | tf_op jit(solution)/shard_map/ppermute | solution.py:28
  853.4 27.0 %collective-permute-start.35 = (f32[4,16,2,260]{3,2,1,0:T(2,128)}, f32[4,16,2,260]{3,2,1,0:T(2,128)}, u32[]{:S(2)}, u32[]{:S(2)}) collective-permute-start(f32[4,16,2,260]{3,2,1,0:T(2,128)} %get-tuple-element.22), channel_id=1, source_target_pairs={{16,0},{32,16},{48,32},{64,48},{80,64},{96,80},{112,96},{17,1},{33... | collective-permute-start | bytes 399368 | tf_op jit(solution)/shard_map/ppermute | solution.py:30
  1157.3 10.6 collective-permute-start.36
  1157.9 10.0 collective-permute-start.37
  1169.3 21.6 %collective-permute-start.38 = (f32[4,16,2,260]{3,2,1,0:T(2,128)}, f32[4,16,2,260]{3,2,1,0:T(2,128)}, u32[]{:S(2)}, u32[]{:S(2)}) collective-permute-start(f32[4,16,2,260]{3,2,1,0:T(2,128)} %get-tuple-element.20), channel_id=1, source_target_pairs={{0,16},{16,32},{32,48},{48,64},{64,80},{80,96},{96,112},{1,17},{17... | collective-permute-start | bytes 399368 | tf_op jit(solution)/shard_map/ppermute | solution.py:28
  1172.9 18.0 %collective-permute-start.39 = (f32[4,16,2,260]{3,2,1,0:T(2,128)}, f32[4,16,2,260]{3,2,1,0:T(2,128)}, u32[]{:S(2)}, u32[]{:S(2)}) collective-permute-start(f32[4,16,2,260]{3,2,1,0:T(2,128)} %get-tuple-element.19), channel_id=1, source_target_pairs={{16,0},{32,16},{48,32},{64,48},{80,64},{96,80},{112,96},{17,1},{33... | collective-permute-start | bytes 399368 | tf_op jit(solution)/shard_map/ppermute | solution.py:30
  1197.8 11.1 collective-permute-start.40
  1197.9 11.0 collective-permute-start.41
  1210.3 23.7 %collective-permute-start.42 = (f32[4,16,2,260]{3,2,1,0:T(2,128)}, f32[4,16,2,260]{3,2,1,0:T(2,128)}, u32[]{:S(2)}, u32[]{:S(2)}) collective-permute-start(f32[4,16,2,260]{3,2,1,0:T(2,128)} %get-tuple-element.18), channel_id=1, source_target_pairs={{0,16},{16,32},{32,48},{48,64},{64,80},{80,96},{96,112},{1,17},{17... | collective-permute-start | bytes 399368 | tf_op jit(solution)/shard_map/ppermute | solution.py:28
  1213.2 20.8 %collective-permute-start.43 = (f32[4,16,2,260]{3,2,1,0:T(2,128)}, f32[4,16,2,260]{3,2,1,0:T(2,128)}, u32[]{:S(2)}, u32[]{:S(2)}) collective-permute-start(f32[4,16,2,260]{3,2,1,0:T(2,128)} %get-tuple-element.17), channel_id=1, source_target_pairs={{16,0},{32,16},{48,32},{64,48},{80,64},{96,80},{112,96},{17,1},{33... | collective-permute-start | bytes 399368 | tf_op jit(solution)/shard_map/ppermute | solution.py:30
  (137 other events, 2234.2 us)
where the time goes:
time: 1320 us; the launch traced here: 1310 us
  other arithmetic  467 us (35%)
  local copies, waits for them, and re-layouts  368 us (28%)
  blocking collectives  240 us (18%)
  starting transfers between devices  149 us (11%)
  waiting for transfers between devices  74 us (6%)
    scatter-add x3, other arithmetic, adjoint_model(): jax.ops.segment_sum(terms, flat_index.reshape(-1), num_segments=WIN * TYP...  260 us
    gather x4, local copies, waits for them, and re-layouts, shards(): values = images.reshape(-1)[flat_index]  181 us
    unnamed x2, blocking collectives  132 us
    scatter-add x9, other arithmetic, adjoint_model(): forcing = [jnp.zeros((channels, cells), jnp.float32).at[:, send_row].add(...  114 us
    ppermute x22, starting transfers between devices, padded(): lax.ppermute(head, axis, [((i + 1) % count, i) for i in range(ends)])  73.2 us
    gather x12, local copies, waits for them, and re-layouts, shards(): jnp.take(state.reshape(channels, cells), send_row, axis=1)  60.2 us
    psum x8, blocking collectives, by_axis(): array = lax.psum(array, axis)  59.2 us
    ppermute x22, starting transfers between devices, padded(): lax.ppermute(tail, axis, [(i, (i + 1) % count) for i in range(ends)])  55.7 us
  transfers between devices with their start and end apart: 46, of which 17 were waited for; matrix products, arithmetic and copies ran while one was open for 13% of the time, Pallas kernels for 0%

commit v1 on v0

v1 whole, which is shorter than its diff:
```python
import functools

import jax
import jax.numpy as jnp
from jax import lax
from jax.experimental import pallas as pl
from jax.experimental.pallas import tpu as pltpu
from jax.sharding import PartitionSpec as P

MESH = pl.DeviceIdType.MESH
F32 = jnp.float32
BF16 = jnp.bfloat16

TYPES = 8
WIN = 3
WT = WIN * TYPES
KPTS = 4
SLOTS = 16
ROWS = 128
N_LAT = 8
N_LON = 16
NDEV = N_LAT * N_LON
NBLK = 32
LEV = 16
CH = 64
LAT = 8
LON = 256
EXT = 16
LANES = 384
NT = (((1,), (1,)), ((), ()))


def split(value):
    high = value.astype(BF16).astype(F32)
    return high, value - high


def mm(left, right):
    return jnp.dot(left, right, preferred_element_type=F32)


def mm_nt(left, right):
    return lax.dot_general(left, right, NT, preferred_element_type=F32)


def place(number):
    return {"lat": number // N_LON, "lon": lax.rem(number, N_LON)}


def pack_rows(rows):
    packed = None
    for r, row in enumerate(rows):
        lane = lax.broadcasted_iota(jnp.int32, (row.shape[0], 128), 1)
        ends = jnp.where(lane < 64, row[:, :128], row[:, 128:])
        moved = pltpu.roll(ends, 4 + 16 * r, axis=1)
        packed = moved if packed is None else jnp.where((lane >> 4) == r, moved, packed)
    return packed


def kernel(
    zonal, merid, op2, opt4, innov, weight, interp, slots, cols, meta_v, count_s, type_s, window_s,
    x_out, r_out,
    winds, field, res, dirn, inc, kp,
    onehot, cweight, live, zrow, yrow, rblk, tsplit,
    colhot, proj, ssum, sext, stage, lgather, lscatter, sacc,
    send_f, send_b, recv_f, recv_b, wown,
    pack_w, pack_x, pack_s, ns_w, ns_x, ns_s, hp_w, hp_x, hp_s, rrv, part,
    a2a_send, a2a_recv, hw_send, hw_recv, hx_send, hx_recv, hs_send, hs_recv,
):
    lat = lax.axis_index("lat")
    lon = lax.axis_index("lon")
    me = lat * N_LON + lon
    barrier = pltpu.get_barrier_semaphore()

    def greet(i, carry):
        pl.semaphore_signal(
            barrier, inc=1, device_id=place(lax.rem(me + i, NDEV)), device_id_type=MESH
        )
        return carry

    lax.fori_loop(1, NDEV, greet, 0)

    north = lax.rem(lat + 1, N_LAT)
    south = lax.rem(lat + N_LAT - 1, N_LAT)
    east = lax.rem(lon + 1, N_LON)
    west = lax.rem(lon + N_LON - 1, N_LON)
    valid_s = jnp.where(lat > 0, 1.0, 0.0).astype(F32)
    valid_n = jnp.where(lat < N_LAT - 1, 1.0, 0.0).astype(F32)

    def halo(low, high, pack, ns, hp, send, recv):
        copies = [
            (high, ns.at[0], north, lon),
            (low, ns.at[1], south, lon),
            (pack, hp.at[0], lat, east),
            (pack, hp.at[1], lat, west),
            (pack, hp.at[2], north, east),
            (pack, hp.at[3], north, west),
            (pack, hp.at[4], south, east),
            (pack, hp.at[5], south, west),
        ]
        return [
            pltpu.make_async_remote_copy(
                src, dst, send.at[i], recv.at[i], device_id={"lat": a, "lon": o}, device_id_type=MESH
            )
            for i, (src, dst, a, o) in enumerate(copies)
        ]

    def halo_w():
        return halo(wown.at[pl.ds(0, 4)], wown.at[pl.ds(4, 4)], pack_w, ns_w, hp_w, hw_send, hw_recv)

    def halo_x():
        return halo(res.at[pl.ds(0, 4)], res.at[pl.ds(4, 4)], pack_x, ns_x, hp_x, hx_send, hx_recv)

    def halo_s():
        return halo(ssum.at[pl.ds(0, 4)], ssum.at[pl.ds(4, 4)], pack_s, ns_s, hp_s, hs_send, hs_recv)

    def sides(hp, base, rows):
        lane = lax.broadcasted_iota(jnp.int32, hp.shape[1:], 1)
        both = jnp.where((lane & 15) < 4, hp[base], hp[base + 1])
        return [pltpu.roll(both, (256 - 16 * r - 4) % 128, axis=1) for r in rows]

    def a2a_start(src, dst, k):
        def go(i, carry):
            to = lax.rem(me + i, NDEV)
            pltpu.make_async_remote_copy(
                src.at[to], dst.at[me], a2a_send.at[k], a2a_recv.at[k],
                device_id=place(to), device_id_type=MESH,
            ).start()
            return carry

        lax.fori_loop(1, NDEV, go, 0)
        dst[me] = src[me]

    def a2a_wait(src, dst, k):
        got = dst.at[pl.ds(0, NDEV - 1)]
        pltpu.make_async_copy(got, got, a2a_recv.at[k]).wait()
        gone = src.at[pl.ds(0, NDEV - 1)]
        pltpu.make_async_copy(gone, gone, a2a_send.at[k]).wait()

    for r in range(LAT):
        wown[r, :LEV, :] = zonal[:, r, :]
        wown[r, LEV:, :] = merid[:, r, :]
    pack_w[...] = pack_rows([wown[r] for r in range(LAT)])

    def tables(b, carry):
        at = pl.ds(pl.multiple_of(b * ROWS, ROWS), ROWS)
        slot = slots[:, at]
        wgt = interp[:, at]
        sender = slot >> 4
        inner = slot & 15
        sub = lax.broadcasted_iota(jnp.int32, (NDEV, ROWS), 0)
        sub16 = lax.broadcasted_iota(jnp.int32, (SLOTS, ROWS), 0)
        for k in range(KPTS):
            lanes = slice(k * ROWS, (k + 1) * ROWS)
            onehot[b, :, lanes] = jnp.where(sub == sender[k : k + 1], 1.0, 0.0).astype(BF16)
            cweight[b, :, lanes] = jnp.where(sub16 == inner[k : k + 1], wgt[k : k + 1], 0.0)
        lane = lax.broadcasted_iota(jnp.int32, (1, ROWS), 1)
        wl = jnp.where(lane < count_s[b], weight[b], 0.0)
        live[b] = wl
        zrow[b] = wl * innov[b]
        yrow[b] = jnp.zeros((1, ROWS), F32)
        return carry

    lax.fori_loop(0, NBLK, tables, 0)
    for n in range(8):
        low = cols[:, n * 256 : (n + 1) * 256] & 127
        sub = lax.broadcasted_iota(jnp.int32, (128, 256), 0)
        colhot[n] = jnp.where(sub == low, 1.0, 0.0).astype(BF16)
    lane32 = lax.broadcasted_iota(jnp.int32, (CH, 32), 1)
    opt_h, opt_l = split(opt4[...])
    opt = jnp.where((lane32 & 8) == 0, opt_h, opt_l).astype(BF16)
    op_h, op_l = split(op2[...])
    opp = jnp.concatenate([op_h, op_l], axis=0).astype(BF16)
    ids = meta_v[1:2, :] * TYPES + meta_v[0:1, :]
    member = jnp.where(lax.broadcasted_iota(jnp.int32, (32, NBLK), 0) == ids, 1.0, 0.0).astype(BF16)
    for r in range(LAT):
        dirn[r] = jnp.zeros((CH, LON), F32)
        inc[r] = jnp.zeros((CH, LON), F32)
    rrv[...] = jnp.ones((1, 128), F32)
    part[...] = jnp.zeros((1, 128), F32)

    pl.semaphore_wait(barrier, NDEV - 1)
    for copy in halo_w():
        copy.start()

    def build_winds():
        for copy in halo_w():
            copy.wait()
        tiles = [None] * EXT
        own = sides(hp_w, 0, range(8))
        low = sides(hp_w, 2, range(4, 8))
        high = sides(hp_w, 4, range(0, 4))
        for e in range(EXT):
            if e < 4:
                main, side, ok = ns_w[0, e], low[e], valid_s
            elif e < 12:
                main, side, ok = wown[e - 4], own[e - 4], None
            else:
                main, side, ok = ns_w[1, e - 12], high[e - 12], valid_n
            both = jnp.concatenate([main, side], axis=1)
            u = both[:LEV]
            v = both[LEV:]
            values = (
                1.0 - jnp.abs(u) - jnp.abs(v),
                jnp.maximum(u, 0.0),
                jnp.maximum(-u, 0.0),
                jnp.maximum(v, 0.0),
                jnp.maximum(-v, 0.0),
            )
            for i, value in enumerate(values):
                winds[i, e] = value if ok is None else value * ok

    def advance(dst, src, lo, hi, adjoint, emit):
        def body(e, carry):
            for var in range(4):
                at = slice(var * LEV, (var + 1) * LEV)
                x = field[src, e, at, :]
                below = field[src, e - 1, at, :]
                above = field[src, e + 1, at, :]
                if adjoint:
                    out = (
                        winds[0, e] * x
                        + pltpu.roll(winds[1, e] * x, LANES - 1, axis=1)
                        + pltpu.roll(winds[2, e] * x, 1, axis=1)
                        + winds[3, e + 1] * above
                        + winds[4, e - 1] * below
                    )
                else:
                    out = (
                        winds[0, e] * x
                        + winds[1, e] * pltpu.roll(x, 1, axis=1)
                        + winds[2, e] * pltpu.roll(x, LANES - 1, axis=1)
                        + winds[3, e] * below
                        + winds[4, e] * above
                    )
                emit(dst, e, at, out)
            return carry

        lax.fori_loop(lo, hi, body, 0)

    def put(dst, e, at, out):
        field[dst, e, at, :] = out

    def project(window, source):
        def body(r, carry):
            high, low = split(source(r))
            both = jnp.concatenate([high, low], axis=0).astype(BF16)
            out = mm(opp, both)
            proj[r, window * TYPES : (window + 1) * TYPES, :] = out[:8] + out[8:]
            return carry

        lax.fori_loop(0, LAT, body, 0)

    def message(dst, row):
        for w in range(WIN):
            dst[:, w, :] = stage[w * 128 : (w + 1) * 128, :].T
        dst[:, 3, :] = jnp.broadcast_to(row, (NDEV, 128))

    def total(recv):
        lanes = jnp.sum(recv[:, 3, :], axis=0, keepdims=True)
        return jnp.broadcast_to(jnp.sum(lanes, axis=1, keepdims=True), (1, 128))

    def wide(row):
        return jnp.concatenate([row, row], axis=1)

    def forward(it):
        pack_x[...] = pack_rows([res[r] for r in range(LAT)])
        for copy in halo_x():
            copy.start()
        project(0, lambda r: res[r])
        for copy in halo_x():
            copy.wait()
        own = sides(hp_x, 0, range(8))
        for r in range(LAT):
            field[0, r + 4, :, :256] = res[r]
            field[0, r + 4, :, 256:] = own[r]
        low = sides(hp_x, 2, range(4, 8))
        high = sides(hp_x, 4, range(0, 4))
        for e in range(4):
            field[0, e, :, :256] = ns_x[0, e] * valid_s
            field[0, e, :, 256:] = low[e] * valid_s
            field[0, e + 12, :, :256] = ns_x[1, e] * valid_n
            field[0, e + 12, :, 256:] = high[e] * valid_n
        advance(1, 0, 1, 15, False, put)
        advance(0, 1, 2, 14, False, put)
        project(1, lambda r: field[0, r + 4, :, :256])
        advance(1, 0, 3, 13, False, put)
        advance(0, 1, 4, 12, False, put)
        project(2, lambda r: field[0, r + 4, :, :256])
        for r in range(LAT):
            value = proj[r]
            pair = jnp.concatenate([value[:, :128], value[:, 128:]], axis=0)
            high, low = split(pair)
            lgather[r * 48 : (r + 1) * 48, :128] = high.astype(BF16)
            lgather[r * 48 : (r + 1) * 48, 128:] = low.astype(BF16)
        for n in range(8):
            hot = colhot[n]
            found = mm(lgather[...], jnp.concatenate([hot, hot], axis=0))
            band = jnp.broadcast_to(cols[:, n * 256 : (n + 1) * 256] >> 7, (WT, 256))
            got = found[:WT]
            for h in range(1, 16):
                got = jnp.where(band == h, found[h * WT : (h + 1) * WT], got)
            for half in range(2):
                for w in range(WIN):
                    stage[pl.ds(w * 128 + 2 * n + half, 8, stride=16), :] = got[
                        w * 8 : (w + 1) * 8, half * 128 : (half + 1) * 128
                    ]
        message(send_f, part[...])
        a2a_start(send_f, recv_f, 0)
        a2a_wait(send_f, recv_f, 0)
        norm = total(recv_f)
        beta = jnp.where(it == 1, jnp.zeros_like(norm), norm / rrv[...])
        rrv[...] = norm
        for w in range(WIN):
            table = recv_f[:, w, :].T
            high, low = split(table)
            for t in range(TYPES):
                at = slice(t * 16, (t + 1) * 16)
                tsplit[w * TYPES + t] = jnp.concatenate([high[at], low[at]], axis=0).astype(BF16)

        def look(b, acc):
            which = window_s[b] * TYPES + type_s[b]
            got = mm(tsplit[which], onehot[b])
            both = (got[:16] + got[16:]) * cweight[b]
            summed = (both[:, :128] + both[:, 128:256]) + (both[:, 256:384] + both[:, 384:])
            y = jnp.sum(summed, axis=0, keepdims=True) + beta * yrow[b]
            yrow[b] = y
            z = live[b] * y
            zrow[b] = z
            return acc + z * y

        quad = lax.fori_loop(0, NBLK, look, jnp.zeros((1, ROWS), F32), unroll=4)

        def turn(r, acc):
            p = res[r] + wide(beta) * dirn[r]
            dirn[r] = p
            return acc + jnp.sum((p * p).reshape(8, 8, LON), axis=0)

        pp = lax.fori_loop(0, LAT, turn, jnp.zeros((8, LON), F32))
        pp = jnp.sum(pp, axis=0, keepdims=True)
        part[...] = quad + pp[:, :128] + pp[:, 128:]

    def outer(it, carry):
        @pl.when(it > 0)
        def _():
            forward(it)

        def spread(b, c):
            z = zrow[b]
            value = cweight[b] * jnp.concatenate([z, z, z, z], axis=1)
            high, low = split(value)
            both = jnp.concatenate([high, low], axis=0).astype(BF16)
            out = mm_nt(both, onehot[b])
            rblk[b] = out[:16] + out[16:]
            return c

        lax.fori_loop(0, NBLK, spread, 0, unroll=4)
        for q in range(SLOTS):
            high, low = split(rblk[:, q, :])
            out = mm(member, high.astype(BF16)) + mm(member, low.astype(BF16))
            for w in range(WIN):
                stage[pl.ds(w * 128 + q, 8, stride=16), :] = out[w * 8 : (w + 1) * 8]
        message(send_b, part[...])
        a2a_start(send_b, recv_b, 1)

        @pl.when(it == 0)
        def _():
            build_winds()

        a2a_wait(send_b, recv_b, 1)
        for w in range(WIN):
            stage[w * 128 : (w + 1) * 128, :] = recv_b[:, w, :].T
        alpha = rrv[...] / total(recv_b)
        for n in range(8):
            halves = []
            for half in range(2):
                halves.append(
                    jnp.concatenate(
                        [stage[pl.ds(w * 128 + 2 * n + half, 8, stride=16), :] for w in range(WIN)],
                        axis=0,
                    )
                )
            high, low = split(jnp.concatenate(halves, axis=1))
            band = jnp.broadcast_to(cols[:, n * 256 : (n + 1) * 256] >> 7, (WT, 256))
            for r in range(LAT):
                for i, value in enumerate((high, low)):
                    pair = jnp.concatenate(
                        [
                            jnp.where(band == 2 * r, value, 0.0),
                            jnp.where(band == 2 * r + 1, value, 0.0),
                        ],
                        axis=0,
                    ).astype(BF16)
                    lscatter[r * 48 : (r + 1) * 48, i * 256 : (i + 1) * 256] = pair
            hot = colhot[n]
            out = mm_nt(lscatter[...], jnp.concatenate([hot, hot], axis=1))
            if n == 0:
                sacc[...] = out
            else:
                sacc[...] += out
        for r in range(LAT):
            ssum[r, :, :128] = sacc[r * 48 : r * 48 + WT, :]
            ssum[r, :, 128:] = sacc[r * 48 + WT : (r + 1) * 48, :]
        pack_s[...] = pack_rows([ssum[r] for r in range(LAT)])
        for copy in halo_s():
            copy.start()
        for copy in halo_s():
            copy.wait()
        own = sides(hp_s, 0, range(8))
        low = sides(hp_s, 2, range(4, 8))
        high = sides(hp_s, 4, range(0, 4))
        for r in range(LAT):
            sext[r + 4, :, :256] = ssum[r]
            sext[r + 4, :, 256:] = own[r]
        for e in range(4):
            sext[e, :, :256] = ns_s[0, e]
            sext[e, :, 256:] = low[e]
            sext[e + 12, :, :256] = ns_s[1, e]
            sext[e + 12, :, 256:] = high[e]

        def forcing(e, window):
            high, low = split(sext[e, window * TYPES : (window + 1) * TYPES, :])
            return mm(opt, jnp.concatenate([high, high, low, low], axis=0).astype(BF16))

        def last(e, c):
            field[0, e] = forcing(e, 2)
            return c

        def middle(e, c):
            field[0, e] += forcing(e, 1)
            return c

        lax.fori_loop(0, EXT, last, 0, unroll=2)
        advance(1, 0, 1, 15, True, put)
        advance(0, 1, 2, 14, True, put)
        lax.fori_loop(2, 14, middle, 0, unroll=2)
        advance(1, 0, 3, 13, True, put)
        advance(0, 1, 4, 12, True, put)

        def result(r):
            return field[0, r + 4, :, :256] + forcing(r + 4, 0)[:, :256]

        @pl.when(it == 0)
        def _():
            def body(r, acc):
                value = result(r)
                res[r] = value
                return acc + jnp.sum((value * value).reshape(8, 8, LON), axis=0)

            acc = lax.fori_loop(0, LAT, body, jnp.zeros((8, LON), F32))
            acc = jnp.sum(acc, axis=0, keepdims=True)
            part[...] = acc[:, :128] + acc[:, 128:]

        @pl.when(it > 0)
        def _():
            scale = wide(alpha)

            def body(r, acc):
                p = dirn[r]
                q = p + result(r)
                x = inc[r] + scale * p
                value = res[r] - scale * q
                inc[r] = x
                res[r] = value
                return acc + jnp.sum((value * value).reshape(8, 8, LON), axis=0)

            acc = lax.fori_loop(0, LAT, body, jnp.zeros((8, LON), F32))
            acc = jnp.sum(acc, axis=0, keepdims=True)
            part[...] = acc[:, :128] + acc[:, 128:]

        return carry

    lax.fori_loop(0, 3, outer, 0)
    x_out[...] = inc[...]
    r_out[...] = res[...]


def shards(
    zonal_wind, merid_wind, operator_rows, innovation, error_weight, interp_weight, obs_slot,
    block_count, block_type, block_window, send_cols,
):
    op2 = jnp.tile(operator_rows, (1, 2))
    opt4 = jnp.tile(operator_rows.T, (1, 4))
    cols = send_cols.reshape(NDEV, SLOTS).T.reshape(1, NDEV * SLOTS)
    meta = jnp.stack([block_type, block_window])
    vm = pl.BlockSpec(memory_space=pltpu.VMEM)
    sm = pl.BlockSpec(memory_space=pltpu.SMEM)
    V = pltpu.VMEM
    dma = pltpu.SemaphoreType.DMA
    x, r = pl.pallas_call(
        kernel,
        out_shape=[jax.ShapeDtypeStruct((LAT, CH, LON), F32)] * 2,
        in_specs=[vm] * 10 + [sm] * 3,
        out_specs=[vm] * 2,
        scratch_shapes=[
            V((5, EXT, LEV, LANES), F32),
            V((2, EXT, CH, LANES), F32),
            V((LAT, CH, LON), F32),
            V((LAT, CH, LON), F32),
            V((LAT, CH, LON), F32),
            V((8, 128), F32),
            V((NBLK, NDEV, KPTS * ROWS), BF16),
            V((NBLK, SLOTS, KPTS * ROWS), F32),
            V((NBLK, 1, ROWS), F32),
            V((NBLK, 1, ROWS), F32),
            V((NBLK, 1, ROWS), F32),
            V((NBLK, SLOTS, NDEV), F32),
            V((WT, 32, NDEV), BF16),
            V((8, 128, 256), BF16),
            V((LAT, WT, LON), F32),
            V((LAT, WT, LON), F32),
            V((EXT, WT, LANES), F32),
            V((WIN * 128, 128), F32),
            V((16 * WT, 256), BF16),
            V((16 * WT, 512), BF16),
            V((16 * WT, 128), F32),
            V((NDEV, 4, 128), F32),
            V((NDEV, 4, 128), F32),
            V((NDEV, 4, 128), F32),
            V((NDEV, 4, 128), F32),
            V((LAT, 2 * LEV, LON), F32),
            V((2 * LEV, 128), F32),
            V((CH, 128), F32),
            V((WT, 128), F32),
            V((2, 4, 2 * LEV, LON), F32),
            V((2, 4, CH, LON), F32),
            V((2, 4, WT, LON), F32),
            V((6, 2 * LEV, 128), F32),
            V((6, CH, 128), F32),
            V((6, WT, 128), F32),
            V((1, 128), F32),
            V((1, 128), F32),
            dma((2,)),
            dma((2,)),
            dma((8,)),
            dma((8,)),
            dma((8,)),
            dma((8,)),
            dma((8,)),
            dma((8,)),
        ],
        compiler_params=pltpu.CompilerParams(
            collective_id=0, has_side_effects=True, vmem_limit_bytes=60 << 20
        ),
        name="cg",
    )(
        zonal_wind, merid_wind, op2, opt4,
        innovation.reshape(NBLK, 1, ROWS), error_weight.reshape(NBLK, 1, ROWS),
        interp_weight, obs_slot, cols, meta, block_count, block_type, block_window,
    )
    shape = (4, LEV, LAT, LON)
    return x.transpose(1, 0, 2).reshape(shape), r.transpose(1, 0, 2).reshape(shape)


def solution(mesh):
    both = ("lat", "lon")
    in_specs = (
        P(None, "lat", "lon"),
        P(None, "lat", "lon"),
        P(),
        P(both),
        P(both),
        P(None, both),
        P(None, both),
        P(both),
        P(both),
        P(both),
        P(both, None),
    )
    out_specs = (P(None, None, "lat", "lon"), P(None, None, "lat", "lon"))
    return jax.shard_map(shards, mesh=mesh, in_specs=in_specs, out_specs=out_specs, check_vma=False)
```

time: 1320 us -> 159 us (0.12)
  other arithmetic: 467 us -> 1.27 us
  local copies, waits for them, and re-layouts: 368 us -> 6.6 us
  blocking collectives: 240 us -> 0 us
  Pallas kernels: 0 us -> 150 us
  starting transfers between devices: 149 us -> 0 us
  waiting for transfers between devices: 74 us -> 0 us
    scatter-add x12 -> x0, other arithmetic: 374 us -> none  [the longest x3 260 us: adjoint_model(): jax.ops.segment_sum(terms, flat_index.reshape(-1), num_segments=WIN * TYP...]
    gather x16 -> x0, local copies, waits for them, and re-layouts: 241 us -> none  [the longest x4 181 us: shards(): values = images.reshape(-1)[flat_index]]
    pallas_call x0 -> x1, Pallas kernels: none -> 150 us  [shards(): pl.pallas_call(kernel, out_shape=[jax.ShapeDtypeStruct((LAT, CH, LON), F3...]
    unnamed x2 -> x0, blocking collectives: 132 us -> none
    ppermute x44 -> x0, starting transfers between devices: 129 us -> none  [the longest x22 73.2 us: padded(): lax.ppermute(head, axis, [((i + 1) % count, i) for i in range(ends)])]
    ppermute x44 -> x0, waiting for transfers between devices: 63.6 us -> none  [the longest x22 51 us: padded(): lax.ppermute(tail, axis, [(i, (i + 1) % count) for i in range(ends)])]
    psum x8 -> x0, blocking collectives: 59.2 us -> none  [by_axis(): array = lax.psum(array, axis)]
    all_to_all x3 -> x0, blocking collectives: 49 us -> none  [the longest x2 30.5 us: adjoint_model(): lax.all_to_all(summed.reshape(WIN * TYPES, recv), LAT_LON, split_axis=1,...]
  transfers between devices with their start and end apart: 46 -> 0, of which waited for: 17 -> 0; matrix products, arithmetic and copies ran while one was open for 13% -> 0% of each run, Pallas kernels for 0% -> 0%
where the time goes in v1:
time: 159 us
  Pallas kernels  150 us (94%)
  local copies, waits for them, and re-layouts  6.6 us (4%)
    pallas_call x1, Pallas kernels, shards(): pl.pallas_call(kernel, out_shape=[jax.ShapeDtypeStruct((LAT, CH, LON), F3...  150 us
    unnamed x13, local copies, waits for them, and re-layouts  4.48 us

profile of v1, /device:TPU:1, one launch (start us, length us, event | category | flops | bytes accessed | tf_op | source)
XLA Modules:
  0.0 158.7 jit_solution(8522757626298863587)
XLA Ops:
  0.6 0.0 copy-start.2
  0.6 0.0 copy-start.3
  0.7 0.0 copy-start.4
  0.7 0.6 copy-done.3
  1.3 0.0 copy-done.4
  1.3 0.6 pad_add_fusion.meta_v
  1.9 0.5 broadcast.9
  2.4 0.0 copy-done.2
  2.4 0.0 copy-start.1
  2.4 0.7 reduce.3
  3.1 0.0 copy-done.1
  3.1 0.7 tile.9.op2
  3.8 0.7 copy.18.opt4
  4.5 0.1 reshape.32
  4.6 0.7 copy.17
  5.3 150.1 %cg.1 = (f32[8,64,256]{2,1,0:T(8,128)}, f32[8,64,256]{2,1,0:T(8,128)}) custom-call(f32[16,8,256]{2,1,0:T(8,128)} %zonal.1, f32[16,8,256]{2,1,0:T(8,128)} %merid.1, f32[8,128]{1,0:T(8,128)} %tile.9.op2, f32[64,32]{1,0:T(8,128)} %copy.18.opt4, f32[32,1,128]{2,1,0:T(1,128)} %bitcast.19, f32[32,1,128]{2,1,0:T(1,128)} %bitcast.20, f32[4,4096]{1,0:T(4,128)} %interp.1, ...), custom_call_target="tpu_custom_call" | custom-call | tf_op jit(solution)/shard_map/cg/pallas_call | solution.py:490
  155.4 0.0 copy-start
  155.4 2.2 %copy.19 = f32[4,16,8,256]{3,2,1,0:T(8,128)} copy(f32[4,16,8,256]{3,1,0,2:T(8,128)} %bitcast.16) | data formatting | bytes 1048576
  157.6 0.0 copy-done
  157.6 1.1 copy.20
  (2 shorter events, 0.0 us)
Async XLA Ops:
  0.6 1.8 %copy-start.2 = (s32[1,2048]{1,0:T(1,128)S(1)}, s32[1,2048]{1,0:T(1,128)}, u32[]{:S(2)}) copy-start(s32[1,2048]{1,0:T(1,128)} %param.21) | copy-start | bytes 24580
  0.6 0.7 copy-start.3
  0.7 0.7 copy-start.4
  2.4 0.7 copy-start.1
  155.4 2.2 %copy-start = (f32[8,64,256]{2,1,0:T(8,128)S(1)}, f32[8,64,256]{2,1,0:T(8,128)}, u32[]{:S(2)}) copy-start(f32[8,64,256]{2,1,0:T(8,128)} %get-tuple-element.5) | copy-start | bytes 1572868

commit v2 on v1

--- a/solution.py
+++ b/solution.py
@@ -43,10 +43,6 @@
     return lax.dot_general(left, right, NT, preferred_element_type=F32)
 
 
-def place(number):
-    return {"lat": number // N_LON, "lon": lax.rem(number, N_LON)}
-
-
 def pack_rows(rows):
     packed = None
     for r, row in enumerate(rows):
@@ -58,9 +54,10 @@
 
 
 def kernel(
-    zonal, merid, op2, opt4, innov, weight, interp, slots, cols, meta_v, count_s, type_s, window_s,
+    zonal, merid, rows_in, innov, weight, interp, slots, cols, type_v, window_v,
+    count_s, type_s, window_s,
     x_out, r_out,
-    winds, field, res, dirn, inc, kp,
+    winds, field, res, dirn, inc, force0, force1, square,
     onehot, cweight, live, zrow, yrow, rblk, tsplit,
     colhot, proj, ssum, sext, stage, lgather, lscatter, sacc,
     send_f, send_b, recv_f, recv_b, wown,
@@ -72,13 +69,25 @@
     me = lat * N_LON + lon
     barrier = pltpu.get_barrier_semaphore()
 
-    def greet(i, carry):
+    lons = [lax.rem(lon + j, N_LON) for j in range(N_LON)]
+
+    def everyone(act):
+        def far(i, carry):
+            a = lax.rem(lat + i, N_LAT)
+            for o in lons:
+                act(a, o)
+            return carry
+
+        lax.fori_loop(1, N_LAT, far, 0)
+        for o in lons[1:]:
+            act(lat, o)
+
+    def greet(a, o):
         pl.semaphore_signal(
-            barrier, inc=1, device_id=place(lax.rem(me + i, NDEV)), device_id_type=MESH
+            barrier, inc=1, device_id={"lat": a, "lon": o}, device_id_type=MESH
         )
-        return carry
-
-    lax.fori_loop(1, NDEV, greet, 0)
+
+    everyone(greet)
 
     north = lax.rem(lat + 1, N_LAT)
     south = lax.rem(lat + N_LAT - 1, N_LAT)
@@ -120,15 +129,13 @@
         return [pltpu.roll(both, (256 - 16 * r - 4) % 128, axis=1) for r in rows]
 
     def a2a_start(src, dst, k):
-        def go(i, carry):
-            to = lax.rem(me + i, NDEV)
+        def go(a, o):
             pltpu.make_async_remote_copy(
-                src.at[to], dst.at[me], a2a_send.at[k], a2a_recv.at[k],
-                device_id=place(to), device_id_type=MESH,
+                src.at[a * N_LON + o], dst.at[me], a2a_send.at[k], a2a_recv.at[k],
+                device_id={"lat": a, "lon": o}, device_id_type=MESH,
             ).start()
-            return carry
-
-        lax.fori_loop(1, NDEV, go, 0)
+
+        everyone(go)
         dst[me] = src[me]
 
     def a2a_wait(src, dst, k):
@@ -161,17 +168,21 @@
         yrow[b] = jnp.zeros((1, ROWS), F32)
         return carry
 
-    lax.fori_loop(0, NBLK, tables, 0)
+    lax.fori_loop(0, NBLK, tables, 0, unroll=2)
     for n in range(8):
-        low = cols[:, n * 256 : (n + 1) * 256] & 127
-        sub = lax.broadcasted_iota(jnp.int32, (128, 256), 0)
+        low = cols[:, n * 256 : (n + 1) * 256] & 255
+        sub = lax.broadcasted_iota(jnp.int32, (LON, 256), 0)
         colhot[n] = jnp.where(sub == low, 1.0, 0.0).astype(BF16)
     lane32 = lax.broadcasted_iota(jnp.int32, (CH, 32), 1)
-    opt_h, opt_l = split(opt4[...])
+    square[...] = jnp.zeros_like(square)
+    for i in range(4):
+        square[i * TYPES : (i + 1) * TYPES, :CH] = rows_in[...]
+    opt_h, opt_l = split(square[...].T[:CH, :32])
     opt = jnp.where((lane32 & 8) == 0, opt_h, opt_l).astype(BF16)
-    op_h, op_l = split(op2[...])
+    op1 = square[:TYPES, :]
+    op_h, op_l = split(op1 + pltpu.roll(op1, CH, axis=1))
     opp = jnp.concatenate([op_h, op_l], axis=0).astype(BF16)
-    ids = meta_v[1:2, :] * TYPES + meta_v[0:1, :]
+    ids = window_v[...] * TYPES + type_v[...]
     member = jnp.where(lax.broadcasted_iota(jnp.int32, (32, NBLK), 0) == ids, 1.0, 0.0).astype(BF16)
     for r in range(LAT):
         dirn[r] = jnp.zeros((CH, LON), F32)
@@ -210,7 +221,7 @@
             for i, value in enumerate(values):
                 winds[i, e] = value if ok is None else value * ok
 
-    def advance(dst, src, lo, hi, adjoint, emit):
+    def advance(dst, src, lo, hi, adjoint, unroll, extra=None):
         def body(e, carry):
             for var in range(4):
                 at = slice(var * LEV, (var + 1) * LEV)
@@ -233,13 +244,10 @@
                         + winds[3, e] * below
                         + winds[4, e] * above
                     )
-                emit(dst, e, at, out)
+                field[dst, e, at, :] = out if extra is None else out + extra[e, at, :]
             return carry
 
-        lax.fori_loop(lo, hi, body, 0)
-
-    def put(dst, e, at, out):
-        field[dst, e, at, :] = out
+        lax.fori_loop(lo, hi, body, 0, unroll=unroll)
 
     def project(window, source):
         def body(r, carry):
@@ -249,7 +257,7 @@
             proj[r, window * TYPES : (window + 1) * TYPES, :] = out[:8] + out[8:]
             return carry
 
-        lax.fori_loop(0, LAT, body, 0)
+        lax.fori_loop(0, LAT, body, 0, unroll=4)
 
     def message(dst, row):
         for w in range(WIN):
@@ -268,12 +276,16 @@
         for copy in halo_x():
             copy.start()
         project(0, lambda r: res[r])
-        for copy in halo_x():
+        copies = halo_x()
+        for copy in copies[2:4]:
             copy.wait()
         own = sides(hp_x, 0, range(8))
         for r in range(LAT):
             field[0, r + 4, :, :256] = res[r]
             field[0, r + 4, :, 256:] = own[r]
+        advance(1, 0, 5, 11, False, 3)
+        for copy in copies[:2] + copies[4:]:
+            copy.wait()
         low = sides(hp_x, 2, range(4, 8))
         high = sides(hp_x, 4, range(0, 4))
         for e in range(4):
@@ -281,25 +293,22 @@
             field[0, e, :, 256:] = low[e] * valid_s
             field[0, e + 12, :, :256] = ns_x[1, e] * valid_n
             field[0, e + 12, :, 256:] = high[e] * valid_n
-        advance(1, 0, 1, 15, False, put)
-        advance(0, 1, 2, 14, False, put)
+        advance(1, 0, 1, 5, False, 4)
+        advance(1, 0, 11, 15, False, 4)
+        advance(0, 1, 2, 14, False, 6)
         project(1, lambda r: field[0, r + 4, :, :256])
-        advance(1, 0, 3, 13, False, put)
-        advance(0, 1, 4, 12, False, put)
+        advance(1, 0, 3, 13, False, 5)
+        advance(0, 1, 4, 12, False, 4)
         project(2, lambda r: field[0, r + 4, :, :256])
         for r in range(LAT):
-            value = proj[r]
-            pair = jnp.concatenate([value[:, :128], value[:, 128:]], axis=0)
-            high, low = split(pair)
-            lgather[r * 48 : (r + 1) * 48, :128] = high.astype(BF16)
-            lgather[r * 48 : (r + 1) * 48, 128:] = low.astype(BF16)
+            lgather[r * 48 : (r + 1) * 48, :] = jnp.concatenate(split(proj[r]), axis=0).astype(BF16)
         for n in range(8):
-            hot = colhot[n]
-            found = mm(lgather[...], jnp.concatenate([hot, hot], axis=0))
-            band = jnp.broadcast_to(cols[:, n * 256 : (n + 1) * 256] >> 7, (WT, 256))
-            got = found[:WT]
-            for h in range(1, 16):
-                got = jnp.where(band == h, found[h * WT : (h + 1) * WT], got)
+            found = mm(lgather[...], colhot[n])
+            band = jnp.broadcast_to(cols[:, n * 256 : (n + 1) * 256] >> 8, (WT, 256))
+            got = found[:WT] + found[WT : 2 * WT]
+            for r in range(1, LAT):
+                at = r * 2 * WT
+                got = jnp.where(band == r, found[at : at + WT] + found[at + WT : at + 2 * WT], got)
             for half in range(2):
                 for w in range(WIN):
                     stage[pl.ds(w * 128 + 2 * n + half, 8, stride=16), :] = got[
@@ -329,7 +338,7 @@
             zrow[b] = z
             return acc + z * y
 
-        quad = lax.fori_loop(0, NBLK, look, jnp.zeros((1, ROWS), F32), unroll=4)
+        quad = lax.fori_loop(0, NBLK, look, jnp.zeros((1, ROWS), F32), unroll=8)
 
         def turn(r, acc):
             p = res[r] + wide(beta) * dirn[r]
@@ -354,7 +363,7 @@
             rblk[b] = out[:16] + out[16:]
             return c
 
-        lax.fori_loop(0, NBLK, spread, 0, unroll=4)
+        lax.fori_loop(0, NBLK, spread, 0, unroll=8)
         for q in range(SLOTS):
             high, low = split(rblk[:, q, :])
             out = mm(member, high.astype(BF16)) + mm(member, low.astype(BF16))
@@ -381,64 +390,71 @@
                     )
                 )
             high, low = split(jnp.concatenate(halves, axis=1))
-            band = jnp.broadcast_to(cols[:, n * 256 : (n + 1) * 256] >> 7, (WT, 256))
+            band = jnp.broadcast_to(cols[:, n * 256 : (n + 1) * 256] >> 8, (WT, 256))
             for r in range(LAT):
-                for i, value in enumerate((high, low)):
-                    pair = jnp.concatenate(
-                        [
-                            jnp.where(band == 2 * r, value, 0.0),
-                            jnp.where(band == 2 * r + 1, value, 0.0),
-                        ],
-                        axis=0,
-                    ).astype(BF16)
-                    lscatter[r * 48 : (r + 1) * 48, i * 256 : (i + 1) * 256] = pair
-            hot = colhot[n]
-            out = mm_nt(lscatter[...], jnp.concatenate([hot, hot], axis=1))
+                here = band == r
+                lscatter[r * 48 : (r + 1) * 48, :] = jnp.concatenate(
+                    [jnp.where(here, high, 0.0), jnp.where(here, low, 0.0)], axis=0
+                ).astype(BF16)
+            out = mm_nt(lscatter[...], colhot[n])
             if n == 0:
                 sacc[...] = out
             else:
                 sacc[...] += out
         for r in range(LAT):
-            ssum[r, :, :128] = sacc[r * 48 : r * 48 + WT, :]
-            ssum[r, :, 128:] = sacc[r * 48 + WT : (r + 1) * 48, :]
+            ssum[r] = sacc[r * 48 : r * 48 + WT, :] + sacc[r * 48 + WT : (r + 1) * 48, :]
         pack_s[...] = pack_rows([ssum[r] for r in range(LAT)])
-        for copy in halo_s():
+        copies = halo_s()
+        for copy in copies:
             copy.start()
-        for copy in halo_s():
+
+        def forcing(value):
+            high, low = split(value)
+            return mm(opt, jnp.concatenate([high, high, low, low], axis=0).astype(BF16))
+
+        def nearest(r, c):
+            force0[r] = forcing(ssum[r, :TYPES, :])
+            return c
+
+        def middle(e, c):
+            force1[e] = forcing(sext[e, TYPES : 2 * TYPES, :])
+            return c
+
+        def last(e, c):
+            field[0, e] = forcing(sext[e, 2 * TYPES :, :])
+            return c
+
+        lax.fori_loop(0, LAT, nearest, 0, unroll=4)
+        for copy in copies[2:4]:
             copy.wait()
         own = sides(hp_s, 0, range(8))
-        low = sides(hp_s, 2, range(4, 8))
-        high = sides(hp_s, 4, range(0, 4))
         for r in range(LAT):
             sext[r + 4, :, :256] = ssum[r]
             sext[r + 4, :, 256:] = own[r]
+        lax.fori_loop(4, 12, last, 0, unroll=4)
+        lax.fori_loop(4, 12, middle, 0, unroll=4)
+        advance(1, 0, 5, 11, True, 3)
+        for copy in copies[:2] + copies[4:]:
+            copy.wait()
+        low = sides(hp_s, 2, range(4, 8))
+        high = sides(hp_s, 4, range(0, 4))
         for e in range(4):
             sext[e, :, :256] = ns_s[0, e]
             sext[e, :, 256:] = low[e]
             sext[e + 12, :, :256] = ns_s[1, e]
             sext[e + 12, :, 256:] = high[e]
-
-        def forcing(e, window):
-            high, low = split(sext[e, window * TYPES : (window + 1) * TYPES, :])
-            return mm(opt, jnp.concatenate([high, high, low, low], axis=0).astype(BF16))
-
-        def last(e, c):
-            field[0, e] = forcing(e, 2)
-            return c
-
-        def middle(e, c):
-            field[0, e] += forcing(e, 1)
-            return c
-
-        lax.fori_loop(0, EXT, last, 0, unroll=2)
-        advance(1, 0, 1, 15, True, put)
-        advance(0, 1, 2, 14, True, put)
-        lax.fori_loop(2, 14, middle, 0, unroll=2)
-        advance(1, 0, 3, 13, True, put)
-        advance(0, 1, 4, 12, True, put)
+        lax.fori_loop(0, 4, last, 0, unroll=4)
+        lax.fori_loop(12, 16, last, 0, unroll=4)
+        lax.fori_loop(2, 4, middle, 0, unroll=2)
+        lax.fori_loop(12, 14, middle, 0, unroll=2)
+        advance(1, 0, 1, 5, True, 4)
+        advance(1, 0, 11, 15, True, 4)
+        advance(0, 1, 2, 14, True, 6, force1)
+        advance(1, 0, 3, 13, True, 5)
+        advance(0, 1, 4, 12, True, 4)
 
         def result(r):
-            return field[0, r + 4, :, :256] + forcing(r + 4, 0)[:, :256]
+            return field[0, r + 4, :, :256] + force0[r]
 
         @pl.when(it == 0)
         def _():
@@ -479,10 +495,7 @@
     zonal_wind, merid_wind, operator_rows, innovation, error_weight, interp_weight, obs_slot,
     block_count, block_type, block_window, send_cols,
 ):
-    op2 = jnp.tile(operator_rows, (1, 2))
-    opt4 = jnp.tile(operator_rows.T, (1, 4))
     cols = send_cols.reshape(NDEV, SLOTS).T.reshape(1, NDEV * SLOTS)
-    meta = jnp.stack([block_type, block_window])
     vm = pl.BlockSpec(memory_space=pltpu.VMEM)
     sm = pl.BlockSpec(memory_space=pltpu.SMEM)
     V = pltpu.VMEM
@@ -498,7 +511,9 @@
             V((LAT, CH, LON), F32),
             V((LAT, CH, LON), F32),
             V((LAT, CH, LON), F32),
-            V((8, 128), F32),
+            V((LAT, CH, LON), F32),
+            V((EXT, CH, LANES), F32),
+            V((128, 128), F32),
             V((NBLK, NDEV, KPTS * ROWS), BF16),
             V((NBLK, SLOTS, KPTS * ROWS), F32),
             V((NBLK, 1, ROWS), F32),
@@ -506,14 +521,14 @@
             V((NBLK, 1, ROWS), F32),
             V((NBLK, SLOTS, NDEV), F32),
             V((WT, 32, NDEV), BF16),
-            V((8, 128, 256), BF16),
+            V((8, LON, 256), BF16),
             V((LAT, WT, LON), F32),
             V((LAT, WT, LON), F32),
             V((EXT, WT, LANES), F32),
             V((WIN * 128, 128), F32),
             V((16 * WT, 256), BF16),
-            V((16 * WT, 512), BF16),
-            V((16 * WT, 128), F32),
+            V((16 * WT, 256), BF16),
+            V((16 * WT, 256), F32),
             V((NDEV, 4, 128), F32),
             V((NDEV, 4, 128), F32),
             V((NDEV, 4, 128), F32),
@@ -544,9 +559,10 @@
         ),
         name="cg",
     )(
-        zonal_wind, merid_wind, op2, opt4,
+        zonal_wind, merid_wind, operator_rows,
         innovation.reshape(NBLK, 1, ROWS), error_weight.reshape(NBLK, 1, ROWS),
-        interp_weight, obs_slot, cols, meta, block_count, block_type, block_window,
+        interp_weight, obs_slot, cols, block_type.reshape(1, NBLK), block_window.reshape(1, NBLK),
+        block_count, block_type, block_window,
     )
     shape = (4, LEV, LAT, LON)
     return x.transpose(1, 0, 2).reshape(shape), r.transpose(1, 0, 2).reshape(shape)

time: 159 us -> 120 us (0.75)
  Pallas kernels: 150 us -> 114 us
  local copies, waits for them, and re-layouts: 6.6 us -> 4.74 us
    pallas_call x1, Pallas kernels: 150 us -> 114 us  [shards(): pl.pallas_call(kernel, out_shape=[jax.ShapeDtypeStruct((LAT, CH, LON), F3...]
    unnamed x13 -> x7, local copies, waits for them, and re-layouts: 4.48 us -> 3.99 us
where the time goes in v2:
time: 120 us
  Pallas kernels  114 us (95%)
  local copies, waits for them, and re-layouts  4.74 us (4%)
    pallas_call x1, Pallas kernels, shards(): pl.pallas_call(kernel, out_shape=[jax.ShapeDtypeStruct((LAT, CH, LON), F3...  114 us
    unnamed x7, local copies, waits for them, and re-layouts  3.99 us

profile of v2, /device:TPU:1, one launch (start us, length us, event | category | flops | bytes accessed | tf_op | source)
XLA Modules:
  0.0 119.9 jit_solution(15452136461663343935)
XLA Ops:
  0.6 0.0 copy-start.1
  0.6 0.5 broadcast.3
  1.2 0.2 copy-done.1
  1.3 0.7 reduce.3
  2.0 0.1 reshape.30
  2.1 0.7 copy.16
  2.8 113.8 %cg.1 = (f32[8,64,256]{2,1,0:T(8,128)}, f32[8,64,256]{2,1,0:T(8,128)}) custom-call(f32[16,8,256]{2,1,0:T(8,128)} %zonal.1, f32[16,8,256]{2,1,0:T(8,128)} %merid.1, f32[8,64]{1,0:T(8,128)} %rows_in.1, f32[32,1,128]{2,1,0:T(1,128)} %bitcast.16, f32[32,1,128]{2,1,0:T(1,128)} %bitcast.17, f32[4,4096]{1,0:T(4,128)} %interp.1, s32[4,4096]{1,0:T(4,128)} %slots.1, ...), custom_call_target="tpu_custom_call" | custom-call | tf_op jit(solution)/shard_map/cg/pallas_call | solution.py:503
  116.6 0.0 copy-start
  116.6 2.2 %copy.17 = f32[4,16,8,256]{3,2,1,0:T(8,128)} copy(f32[4,16,8,256]{3,1,0,2:T(8,128)} %bitcast.13) | data formatting | bytes 1048576
  118.8 0.0 copy-done
  118.8 1.1 copy.18
Async XLA Ops:
  0.6 0.7 copy-start.1
  116.6 2.2 %copy-start = (f32[8,64,256]{2,1,0:T(8,128)S(1)}, f32[8,64,256]{2,1,0:T(8,128)}, u32[]{:S(2)}) copy-start(f32[8,64,256]{2,1,0:T(8,128)} %get-tuple-element.5) | copy-start | bytes 1572868

commit v3 on v2

v3 whole, which is shorter than its diff:
```python
import functools

import jax
import jax.numpy as jnp
from jax import lax
from jax.experimental import pallas as pl
from jax.experimental.pallas import tpu as pltpu
from jax.sharding import PartitionSpec as P

MESH = pl.DeviceIdType.MESH
F32 = jnp.float32
BF16 = jnp.bfloat16

TYPES = 8
WIN = 3
WT = WIN * TYPES
KPTS = 4
SLOTS = 16
ROWS = 128
N_LAT = 8
N_LON = 16
NDEV = N_LAT * N_LON
NBLK = 32
LEV = 16
CH = 64
LAT = 8
LON = 256
EXT = 24
MID = 16
LANES = 384
NT = (((1,), (1,)), ((), ()))


def split(value):
    high = value.astype(BF16).astype(F32)
    return high, value - high


def mm(left, right):
    return jnp.dot(left, right, preferred_element_type=F32)


def mm_nt(left, right):
    return lax.dot_general(left, right, NT, preferred_element_type=F32)


def pack_rows(rows):
    packed = None
    for r, row in enumerate(rows):
        lane = lax.broadcasted_iota(jnp.int32, (row.shape[0], 128), 1)
        ends = jnp.where(lane < 64, row[:, :128], row[:, 128:])
        moved = pltpu.roll(ends, (8 + 16 * r) % 128, axis=1)
        packed = moved if packed is None else jnp.where((lane >> 4) == r, moved, packed)
    return packed


def offsets():
    steps = [
        (dx, dc, dy, dz)
        for dx in range(4) for dc in range(2) for dy in range(4) for dz in range(4)
    ][1:]
    return sorted(steps, key=lambda t: -sum(min(d, 4 - d) for d in (t[0], t[2], t[3])))


def kernel(
    zonal, merid, rows_in, innov, weight, interp, slots, cols, type_v, window_v,
    count_s, type_s, window_s,
    x_out, r_out,
    winds, field, res, dirn, inc, force0, force1, square, colq,
    onehot, cweight, live, zrow, yrow, rblk, tsplit,
    colhot, proj, ssum, sside, stage, lgather, lscatter, sacc,
    send_f, send_b, recv_f, recv_b, wown,
    pack_w, pack_s, ns_w, ns_s, hp_w, hp_s, rrv, part, betav,
    a2a_send, a2a_recv, hw_send, hw_recv, hs_send, hs_recv,
):
    lat = lax.axis_index("lat")
    lon = lax.axis_index("lon")
    me = lat * N_LON + lon
    barrier = pltpu.get_barrier_semaphore()

    x, core = lat // 2, lax.rem(lat, 2)
    y, z = lon // 4, lax.rem(lon, 4)
    lats = {
        (dx, dc): lax.rem(x + dx, 4) * 2 + lax.rem(core + dc, 2)
        for dx in range(4) for dc in range(2)
    }
    lons = {
        (dy, dz): lax.rem(y + dy, 4) * 4 + lax.rem(z + dz, 4)
        for dy in range(4) for dz in range(4)
    }

    def everyone(act):
        for dx, dc, dy, dz in offsets():
            act(lats[dx, dc], lons[dy, dz])

    def plain(a, o):
        return a * N_LON + o

    def swapped(a, o):
        return lax.rem(o, 8) * 16 + a * 2 + o // 8

    def greet(a, o):
        pl.semaphore_signal(
            barrier, inc=1, device_id={"lat": a, "lon": o}, device_id_type=MESH
        )

    everyone(greet)

    north = lax.rem(lat + 1, N_LAT)
    south = lax.rem(lat + N_LAT - 1, N_LAT)
    east = lax.rem(lon + 1, N_LON)
    west = lax.rem(lon + N_LON - 1, N_LON)
    valid_s = jnp.where(lat > 0, 1.0, 0.0).astype(F32)
    valid_n = jnp.where(lat < N_LAT - 1, 1.0, 0.0).astype(F32)

    def to(src, dst, a, o, send, recv):
        return pltpu.make_async_remote_copy(
            src, dst, send, recv, device_id={"lat": a, "lon": o}, device_id_type=MESH
        )

    def edges(pack, hp, send, recv):
        targets = [
            (north, east), (north, west), (south, east), (south, west), (lat, east), (lat, west)
        ]
        return [
            to(pack, hp.at[i], a, o, send.at[i], recv.at[i]) for i, (a, o) in enumerate(targets)
        ]

    def halo_w():
        return edges(pack_w, hp_w, hw_send, hw_recv) + [
            to(wown, ns_w.at[0], north, lon, hw_send.at[6], hw_recv.at[6]),
            to(wown, ns_w.at[1], south, lon, hw_send.at[7], hw_recv.at[7]),
        ]

    def halo_s(deep):
        copies = edges(pack_s, hp_s, hs_send, hs_recv)
        k = 6
        for w, count in ((2, 8 if deep else 4), (1, 6 if deep else 2), (0, 4 if deep else 0)):
            if count == 0:
                continue
            high = pl.ds(w * LAT + LAT - count, count)
            low = pl.ds(w * LAT, count)
            copies.append(to(ssum.at[high], ns_s.at[0, high], north, lon, hs_send.at[k], hs_recv.at[k]))
            copies.append(
                to(ssum.at[low], ns_s.at[1, low], south, lon, hs_send.at[k + 1], hs_recv.at[k + 1])
            )
            k += 2
        return copies

    def sides(hp, base):
        lane = lax.broadcasted_iota(jnp.int32, hp.shape[1:], 1)
        both = jnp.where((lane & 15) < 8, hp[base], hp[base + 1])
        return [pltpu.roll(both, (256 - 16 * r - 8) % 128, axis=1) for r in range(LAT)]

    def a2a_start(src, dst, k, row_of, mine):
        def go(a, o):
            to(
                src.at[row_of(a, o)], dst.at[mine], a, o, a2a_send.at[k], a2a_recv.at[k]
            ).start()

        everyone(go)
        dst[mine] = src[row_of(lat, lon)]

    def a2a_wait(src, dst, k):
        got = dst.at[pl.ds(0, NDEV - 1)]
        pltpu.make_async_copy(got, got, a2a_recv.at[k]).wait()
        gone = src.at[pl.ds(0, NDEV - 1)]
        pltpu.make_async_copy(gone, gone, a2a_send.at[k]).wait()

    for r in range(LAT):
        wown[r, :LEV, :] = zonal[:, r, :]
        wown[r, LEV:, :] = merid[:, r, :]
    pack_w[...] = pack_rows([wown[r] for r in range(LAT)])

    def tables(b, carry):
        at = pl.ds(pl.multiple_of(b * ROWS, ROWS), ROWS)
        slot = slots[:, at]
        wgt = interp[:, at]
        sender = slot >> 4
        inner = slot & 15
        sub = lax.broadcasted_iota(jnp.int32, (NDEV, ROWS), 0)
        sub16 = lax.broadcasted_iota(jnp.int32, (SLOTS, ROWS), 0)
        for k in range(KPTS):
            lanes = slice(k * ROWS, (k + 1) * ROWS)
            onehot[b, :, lanes] = jnp.where(sub == sender[k : k + 1], 1.0, 0.0).astype(BF16)
            cweight[b, :, lanes] = jnp.where(sub16 == inner[k : k + 1], wgt[k : k + 1], 0.0)
        lane = lax.broadcasted_iota(jnp.int32, (1, ROWS), 1)
        wl = jnp.where(lane < count_s[b], weight[b], 0.0)
        live[b] = wl
        zrow[b] = wl * innov[b]
        yrow[b] = jnp.zeros((1, ROWS), F32)
        return carry

    lax.fori_loop(0, NBLK, tables, 0, unroll=2)
    raw = jnp.concatenate([cols[:, a * 128 : (a + 1) * 128] for a in range(16)], axis=0).astype(F32)
    sub16 = lax.broadcasted_iota(jnp.int32, (16, 128), 0)
    lane16 = lax.broadcasted_iota(jnp.int32, (16, 128), 1) & 15
    slanted = pltpu.roll(raw, 0, axis=1, stride=1, stride_axis=0)
    for q in range(SLOTS):
        moved = pltpu.roll(slanted, (128 - q) % 128, axis=1)
        kept = jnp.where(lane16 == sub16, moved, 0.0)
        colq[q : q + 1, :] = jnp.sum(kept, axis=0, keepdims=True).astype(jnp.int32)

    def columns(n):
        return jnp.concatenate([colq[2 * n : 2 * n + 1, :], colq[2 * n + 1 : 2 * n + 2, :]], axis=1)

    for n in range(8):
        low = columns(n) & 255
        sub = lax.broadcasted_iota(jnp.int32, (LON, 256), 0)
        colhot[n] = jnp.where(sub == low, 1.0, 0.0).astype(BF16)
    lane32 = lax.broadcasted_iota(jnp.int32, (CH, 32), 1)
    square[...] = jnp.zeros_like(square)
    for i in range(4):
        square[i * TYPES : (i + 1) * TYPES, :CH] = rows_in[...]
    opt_h, opt_l = split(square[...].T[:CH, :32])
    opt = jnp.where((lane32 & 8) == 0, opt_h, opt_l).astype(BF16)
    op1 = square[:TYPES, :]
    op_h, op_l = split(op1 + pltpu.roll(op1, CH, axis=1))
    opp = jnp.concatenate([op_h, op_l], axis=0).astype(BF16)
    ids = window_v[...] * TYPES + type_v[...]
    member = jnp.where(lax.broadcasted_iota(jnp.int32, (32, NBLK), 0) == ids, 1.0, 0.0).astype(BF16)
    def clear(r, carry):
        dirn[r] = jnp.zeros((CH, LANES), F32)
        dirn[r + LAT] = jnp.zeros((CH, LANES), F32)
        inc[r] = jnp.zeros((CH, LON), F32)
        return carry

    lax.fori_loop(0, LAT, clear, 0)
    rrv[...] = jnp.ones((1, 128), F32)
    part[...] = jnp.zeros((1, 128), F32)

    pl.semaphore_wait(barrier, NDEV - 1)
    for copy in halo_w():
        copy.start()

    def build_winds():
        for copy in halo_w():
            copy.wait()
        side = sides(hp_w, 0) + sides(hp_w, 4) + sides(hp_w, 2)
        for g in range(EXT):
            if g < 8:
                main, ok = ns_w[0, g], valid_s
            elif g < 16:
                main, ok = wown[g - 8], None
            else:
                main, ok = ns_w[1, g - 16], valid_n
            side_g = side[g]
            both = jnp.concatenate([main, side_g], axis=1)
            u = both[:LEV]
            v = both[LEV:]
            values = (
                1.0 - jnp.abs(u) - jnp.abs(v),
                jnp.maximum(u, 0.0),
                jnp.maximum(-u, 0.0),
                jnp.maximum(v, 0.0),
                jnp.maximum(-v, 0.0),
            )
            for i, value in enumerate(values):
                winds[i, g] = value if ok is None else value * ok

    def advance(dst, src, shift, lo, hi, adjoint, unroll, extra=None):
        def body(g, carry):
            for var in range(4):
                at = slice(var * LEV, (var + 1) * LEV)
                mid = src[g - shift, at, :]
                below = src[g - shift - 1, at, :]
                above = src[g - shift + 1, at, :]
                if adjoint:
                    out = (
                        winds[0, g] * mid
                        + pltpu.roll(winds[1, g] * mid, LANES - 1, axis=1)
                        + pltpu.roll(winds[2, g] * mid, 1, axis=1)
                        + winds[3, g + 1] * above
                        + winds[4, g - 1] * below
                    )
                else:
                    out = (
                        winds[0, g] * mid
                        + winds[1, g] * pltpu.roll(mid, 1, axis=1)
                        + winds[2, g] * pltpu.roll(mid, LANES - 1, axis=1)
                        + winds[3, g] * below
                        + winds[4, g] * above
                    )
                dst[g, at, :] = out if extra is None else out + extra[g, at, :]
            return carry

        lax.fori_loop(lo, hi, body, 0, unroll=unroll)

    def project(window, source):
        def body(r, carry):
            high, low = split(source(r))
            both = jnp.concatenate([high, low], axis=0).astype(BF16)
            out = mm(opp, both)
            proj[r, window * TYPES : (window + 1) * TYPES, :] = out[:8] + out[8:]
            return carry

        lax.fori_loop(0, LAT, body, 0, unroll=4)

    def message(dst, row):
        for w in range(WIN):
            dst[:, w, :] = stage[w * 128 : (w + 1) * 128, :].T
        dst[:, 3, :] = jnp.broadcast_to(row, (NDEV, 128))

    def total(recv):
        lanes = jnp.sum(recv[:, 3, :], axis=0, keepdims=True)
        return jnp.broadcast_to(jnp.sum(lanes, axis=1, keepdims=True), (1, 128))

    def full(row):
        return jnp.concatenate([row, row, row], axis=1)

    def own_squares(value):
        own = value[:, :LON]
        return jnp.sum((own * own).reshape(8, 8, LON), axis=0)

    def forward(it):
        ping, pong = field.at[0], field.at[1]
        project(0, lambda r: res[r + 4, :, :LON])
        advance(pong, res, 4, 5, 19, False, 7)
        advance(ping, pong, 0, 6, 18, False, 6)
        project(1, lambda r: ping[r + 8, :, :LON])
        advance(pong, ping, 0, 7, 17, False, 5)
        advance(ping, pong, 0, 8, 16, False, 4)
        project(2, lambda r: ping[r + 8, :, :LON])
        for r in range(LAT):
            lgather[r * 48 : (r + 1) * 48, :] = jnp.concatenate(split(proj[r]), axis=0).astype(BF16)
        for n in range(8):
            found = mm(lgather[...], colhot[n])
            band = jnp.broadcast_to(columns(n) >> 8, (WT, 256))
            got = found[:WT] + found[WT : 2 * WT]
            for r in range(1, LAT):
                at = r * 2 * WT
                got = jnp.where(band == r, found[at : at + WT] + found[at + WT : at + 2 * WT], got)
            for half in range(2):
                for w in range(WIN):
                    stage[pl.ds(w * 128 + 2 * n + half, 8, stride=16), :] = got[
                        w * 8 : (w + 1) * 8, half * 128 : (half + 1) * 128
                    ]
        message(send_f, part[...])
        a2a_start(send_f, recv_f, 0, swapped, me)
        a2a_wait(send_f, recv_f, 0)
        norm = total(recv_f)
        beta = jnp.where(it == 1, jnp.zeros_like(norm), norm / rrv[...])
        rrv[...] = norm
        for w in range(WIN):
            table = recv_f[:, w, :].T
            high, low = split(table)
            for t in range(TYPES):
                at = slice(t * 16, (t + 1) * 16)
                tsplit[w * TYPES + t] = jnp.concatenate([high[at], low[at]], axis=0).astype(BF16)

        def look(b, acc):
            which = window_s[b] * TYPES + type_s[b]
            got = mm(tsplit[which], onehot[b])
            both = (got[:16] + got[16:]) * cweight[b]
            summed = (both[:, :128] + both[:, 128:256]) + (both[:, 256:384] + both[:, 384:])
            y = jnp.sum(summed, axis=0, keepdims=True) + beta * yrow[b]
            yrow[b] = y
            z = live[b] * y
            zrow[b] = z
            return acc + z * y

        quad = lax.fori_loop(0, NBLK, look, jnp.zeros((1, ROWS), F32), unroll=8)

        def turn(r, acc):
            p = res[r + 4] + full(beta) * dirn[r + 4]
            dirn[r + 4] = p
            return acc + own_squares(p)

        pp = lax.fori_loop(0, LAT, turn, jnp.zeros((8, LON), F32), unroll=2)
        pp = jnp.sum(pp, axis=0, keepdims=True)
        part[...] = quad + pp[:, :128] + pp[:, 128:]
        betav[...] = beta

    def forcing(value):
        high, low = split(value)
        return mm(opt, jnp.concatenate([high, high, low, low], axis=0).astype(BF16))

    def adjoint(it, alpha, deep):
        copies = halo_s(deep)
        for copy in copies:
            copy.start()
        ping, pong = field.at[0], field.at[1]
        into = {2: ping, 1: force1, 0: force0}
        near = {2: 8 if deep else 4, 1: 6 if deep else 2, 0: 4 if deep else 0}

        def own(r, c):
            for w in range(WIN):
                into[w][r + 8, :, :LON] = forcing(ssum[w * LAT + r])
            return c

        def own_side(r, c):
            for w in range(WIN):
                into[w][r + 8, :, LON:] = forcing(sside[r + 8, w * TYPES : (w + 1) * TYPES, :])
            return c

        def outside(w):
            def body(i, c):
                for k, g, r in ((0, 7 - i, 7 - i), (1, 16 + i, i)):
                    into[w][g, :, :LON] = forcing(ns_s[k, w * LAT + r])
                    into[w][g, :, LON:] = forcing(sside[g, w * TYPES : (w + 1) * TYPES, :])
                return c

            if near[w]:
                lax.fori_loop(0, near[w], body, 0, unroll=2)

        lax.fori_loop(0, LAT, own, 0, unroll=2)
        for copy in copies[4:6]:
            copy.wait()
        for r, value in enumerate(sides(hp_s, 4)):
            sside[r + 8] = value
        lax.fori_loop(0, LAT, own_side, 0, unroll=4)
        advance(pong, ping, 0, 9, 15, True, 3)
        for copy in copies[:4]:
            copy.wait()
        for r, value in enumerate(sides(hp_s, 0)):
            sside[r] = value
        for r, value in enumerate(sides(hp_s, 2)):
            sside[r + 16] = value
        for copy in copies[6:]:
            copy.wait()
        for w in (2, 1, 0):
            outside(w)
        if deep:
            advance(pong, ping, 0, 1, 9, True, 4)
            advance(pong, ping, 0, 15, 23, True, 4)
            advance(ping, pong, 0, 2, 22, True, 5, force1)
            advance(pong, ping, 0, 3, 21, True, 6)
            advance(ping, pong, 0, 4, 20, True, 4, force0)
        else:
            advance(pong, ping, 0, 5, 9, True, 4)
            advance(pong, ping, 0, 15, 19, True, 4)
            advance(ping, pong, 0, 6, 18, True, 6, force1)
            advance(pong, ping, 0, 7, 17, True, 5)
            advance(ping, pong, 0, 8, 16, True, 4, force0)
        zero = jnp.zeros((8, LON), F32)

        def done(acc):
            acc = jnp.sum(acc, axis=0, keepdims=True)
            part[...] = acc[:, :128] + acc[:, 128:]

        scale = full(alpha)
        if deep:

            @pl.when(it == 0)
            def _():
                def rim(i, c):
                    e = i + LAT * (i // 4)
                    ok = jnp.where(i < 4, valid_s, valid_n)
                    res[e] = ping[e + 4] * ok
                    return c

                def body(r, acc):
                    value = ping[r + 8]
                    res[r + 4] = value
                    return acc + own_squares(value)

                lax.fori_loop(0, 8, rim, 0)
                done(lax.fori_loop(0, LAT, body, zero, unroll=2))

            @pl.when(it > 0)
            def _():
                def rim(i, c):
                    e = i + LAT * (i // 4)
                    ok = jnp.where(i < 4, valid_s, valid_n)
                    res[e] -= scale * (dirn[e] + ping[e + 4]) * ok
                    return c

                def body(r, acc):
                    p = dirn[r + 4]
                    inc[r] += scale[:, :LON] * p[:, :LON]
                    value = res[r + 4] - scale * (p + ping[r + 8])
                    res[r + 4] = value
                    return acc + own_squares(value)

                lax.fori_loop(0, 8, rim, 0)
                done(lax.fori_loop(0, LAT, body, zero, unroll=2))
        else:
            narrow = scale[:, :LON]

            def body(r, c):
                p = dirn[r + 4, :, :LON]
                x_out[r] = inc[r] + narrow * p
                r_out[r] = res[r + 4, :, :LON] - narrow * (p + ping[r + 8, :, :LON])
                return c

            lax.fori_loop(0, LAT, body, 0, unroll=2)

    def outer(it, carry):
        @pl.when(it > 0)
        def _():
            forward(it)

        def spread(b, c):
            z = zrow[b]
            value = cweight[b] * jnp.concatenate([z, z, z, z], axis=1)
            high, low = split(value)
            both = jnp.concatenate([high, low], axis=0).astype(BF16)
            out = mm_nt(both, onehot[b])
            rblk[b] = out[:16] + out[16:]
            return c

        lax.fori_loop(0, NBLK, spread, 0, unroll=8)
        for q in range(SLOTS):
            high, low = split(rblk[:, q, :])
            out = mm(member, high.astype(BF16)) + mm(member, low.astype(BF16))
            for w in range(WIN):
                stage[pl.ds(w * 128 + q, 8, stride=16), :] = out[w * 8 : (w + 1) * 8]
        message(send_b, part[...])
        a2a_start(send_b, recv_b, 1, plain, swapped(lat, lon))

        @pl.when(it == 0)
        def _():
            build_winds()

        @pl.when(it == 1)
        def _():
            def beyond(i, c):
                e = i + LAT * (i // 4)
                dirn[e] = res[e] + full(betav[...]) * dirn[e]
                return c

            lax.fori_loop(0, 8, beyond, 0)

        a2a_wait(send_b, recv_b, 1)
        for w in range(WIN):
            stage[w * 128 : (w + 1) * 128, :] = recv_b[:, w, :].T
        alpha = rrv[...] / total(recv_b)
        for n in range(8):
            halves = []
            for half in range(2):
                halves.append(
                    jnp.concatenate(
                        [stage[pl.ds(w * 128 + 2 * n + half, 8, stride=16), :] for w in range(WIN)],
                        axis=0,
                    )
                )
            high, low = split(jnp.concatenate(halves, axis=1))
            band = jnp.broadcast_to(columns(n) >> 8, (WT, 256))
            for r in range(LAT):
                here = band == r
                lscatter[r * 48 : (r + 1) * 48, :] = jnp.concatenate(
                    [jnp.where(here, high, 0.0), jnp.where(here, low, 0.0)], axis=0
                ).astype(BF16)
            out = mm_nt(lscatter[...], colhot[n])
            if n == 0:
                sacc[...] = out
            else:
                sacc[...] += out
        for r in range(LAT):
            value = sacc[r * 48 : r * 48 + WT, :] + sacc[r * 48 + WT : (r + 1) * 48, :]
            for w in range(WIN):
                ssum[w * LAT + r] = value[w * TYPES : (w + 1) * TYPES]
        pack_s[...] = pack_rows(
            [jnp.concatenate([ssum[w * LAT + r] for w in range(WIN)], axis=0) for r in range(LAT)]
        )
        @pl.when(it < 2)
        def _():
            adjoint(it, alpha, True)

        @pl.when(it == 2)
        def _():
            adjoint(it, alpha, False)

        return carry

    lax.fori_loop(0, 3, outer, 0)


def shards(
    zonal_wind, merid_wind, operator_rows, innovation, error_weight, interp_weight, obs_slot,
    block_count, block_type, block_window, send_cols,
):
    vm = pl.BlockSpec(memory_space=pltpu.VMEM)
    sm = pl.BlockSpec(memory_space=pltpu.SMEM)
    V = pltpu.VMEM
    dma = pltpu.SemaphoreType.DMA
    x, r = pl.pallas_call(
        kernel,
        out_shape=[jax.ShapeDtypeStruct((LAT, CH, LON), F32)] * 2,
        in_specs=[vm] * 10 + [sm] * 3,
        out_specs=[vm] * 2,
        scratch_shapes=[
            V((5, EXT, LEV, LANES), F32),
            V((2, EXT, CH, LANES), F32),
            V((MID, CH, LANES), F32),
            V((MID, CH, LANES), F32),
            V((LAT, CH, LON), F32),
            V((EXT, CH, LANES), F32),
            V((EXT, CH, LANES), F32),
            V((128, 128), F32),
            V((SLOTS, 128), jnp.int32),
            V((NBLK, NDEV, KPTS * ROWS), BF16),
            V((NBLK, SLOTS, KPTS * ROWS), F32),
            V((NBLK, 1, ROWS), F32),
            V((NBLK, 1, ROWS), F32),
            V((NBLK, 1, ROWS), F32),
            V((NBLK, SLOTS, NDEV), F32),
            V((WT, 32, NDEV), BF16),
            V((8, LON, 256), BF16),
            V((LAT, WT, LON), F32),
            V((WIN * LAT, TYPES, LON), F32),
            V((EXT, WT, 128), F32),
            V((WIN * 128, 128), F32),
            V((16 * WT, 256), BF16),
            V((16 * WT, 256), BF16),
            V((16 * WT, 256), F32),
            V((NDEV, 4, 128), F32),
            V((NDEV, 4, 128), F32),
            V((NDEV, 4, 128), F32),
            V((NDEV, 4, 128), F32),
            V((LAT, 2 * LEV, LON), F32),
            V((2 * LEV, 128), F32),
            V((WT, 128), F32),
            V((2, LAT, 2 * LEV, LON), F32),
            V((2, WIN * LAT, TYPES, LON), F32),
            V((6, 2 * LEV, 128), F32),
            V((6, WT, 128), F32),
            V((1, 128), F32),
            V((1, 128), F32),
            V((1, 128), F32),
            dma((2,)),
            dma((2,)),
            dma((8,)),
            dma((8,)),
            dma((12,)),
            dma((12,)),
        ],
        compiler_params=pltpu.CompilerParams(
            collective_id=0, has_side_effects=True, vmem_limit_bytes=60 << 20
        ),
        name="cg",
    )(
        zonal_wind, merid_wind, operator_rows,
        innovation.reshape(NBLK, 1, ROWS), error_weight.reshape(NBLK, 1, ROWS),
        interp_weight, obs_slot, send_cols, block_type.reshape(1, NBLK), block_window.reshape(1, NBLK),
        block_count, block_type, block_window,
    )
    shape = (4, LEV, LAT, LON)
    return x.transpose(1, 0, 2).reshape(shape), r.transpose(1, 0, 2).reshape(shape)


def solution(mesh):
    both = ("lat", "lon")
    in_specs = (
        P(None, "lat", "lon"),
        P(None, "lat", "lon"),
        P(),
        P(both),
        P(both),
        P(None, both),
        P(None, both),
        P(both),
        P(both),
        P(both),
        P(both, None),
    )
    out_specs = (P(None, None, "lat", "lon"), P(None, None, "lat", "lon"))
    return jax.shard_map(shards, mesh=mesh, in_specs=in_specs, out_specs=out_specs, check_vma=False)
```

time: 120 us -> 107 us (0.89)
  Pallas kernels: 114 us -> 102 us
  local copies, waits for them, and re-layouts: 4.74 us -> 3.3 us
    pallas_call x1, Pallas kernels: 114 us -> 102 us  [shards(): pl.pallas_call(kernel, out_shape=[jax.ShapeDtypeStruct((LAT, CH, LON), F3...]
    unnamed x7 -> x4, local copies, waits for them, and re-layouts: 3.99 us -> 3.3 us
where the time goes in v3:
time: 107 us; the launch traced here: 106 us
  Pallas kernels  102 us (95%)
  local copies, waits for them, and re-layouts  3.3 us (3%)
    pallas_call x1, Pallas kernels, shards(): pl.pallas_call(kernel, out_shape=[jax.ShapeDtypeStruct((LAT, CH, LON), F3...  102 us
    unnamed x4, local copies, waits for them, and re-layouts  3.3 us

profile of v3, /device:TPU:1, one launch (start us, length us, event | category | flops | bytes accessed | tf_op | source)
XLA Modules:
  0.0 106.4 jit_solution(13109111340655668097)
XLA Ops:
  0.6 102.4 %cg.1 = (f32[8,64,256]{2,1,0:T(8,128)}, f32[8,64,256]{2,1,0:T(8,128)}) custom-call(f32[16,8,256]{2,1,0:T(8,128)} %zonal.1, f32[16,8,256]{2,1,0:T(8,128)} %merid.1, f32[8,64]{1,0:T(8,128)} %rows_in.1, f32[32,1,128]{2,1,0:T(1,128)} %bitcast.12, f32[32,1,128]{2,1,0:T(1,128)} %bitcast.13, f32[4,4096]{1,0:T(4,128)} %interp.1, s32[4,4096]{1,0:T(4,128)} %slots.1, ...), custom_call_target="tpu_custom_call" | custom-call | tf_op jit(solution)/shard_map/cg/pallas_call | solution.py:577
  103.1 0.0 copy-start
  103.1 2.2 %copy.13 = f32[4,16,8,256]{3,2,1,0:T(8,128)} copy(f32[4,16,8,256]{3,1,0,2:T(8,128)} %bitcast.11) | data formatting | bytes 1048576
  105.3 0.0 copy-done
  105.3 1.1 %copy.14 = f32[4,16,8,256]{3,2,1,0:T(8,128)} copy(f32[4,16,8,256]{3,1,0,2:T(8,128)S(1)} %bitcast.10) | data formatting | bytes 1048576
Async XLA Ops:
  103.1 2.2 %copy-start = (f32[8,64,256]{2,1,0:T(8,128)S(1)}, f32[8,64,256]{2,1,0:T(8,128)}, u32[]{:S(2)}) copy-start(f32[8,64,256]{2,1,0:T(8,128)} %get-tuple-element.5) | copy-start | bytes 1572868

commit v4 on v3

--- a/solution.py
+++ b/solution.py
@@ -63,16 +63,24 @@
 
 
 def kernel(
-    zonal, merid, rows_in, innov, weight, interp, slots, cols, type_v, window_v,
+    zonal_h, merid_h, interp_h, slots_h, rows_in, innov, weight, cols, type_v, window_v,
     count_s, type_s, window_s,
     x_out, r_out,
-    winds, field, res, dirn, inc, force0, force1, square, colq,
+    zonal, merid, interp, slots, in_sem, winds, field, res, dirn, inc, force0, force1, square, colq,
     onehot, cweight, live, zrow, yrow, rblk, tsplit,
     colhot, proj, ssum, sside, stage, lgather, lscatter, sacc,
     send_f, send_b, recv_f, recv_b, wown,
     pack_w, pack_s, ns_w, ns_s, hp_w, hp_s, rrv, part, betav,
     a2a_send, a2a_recv, hw_send, hw_recv, hs_send, hs_recv,
 ):
+    loads = [
+        pltpu.make_async_copy(src, dst, in_sem.at[i])
+        for i, (src, dst) in enumerate(
+            ((zonal_h, zonal), (merid_h, merid), (interp_h, interp), (slots_h, slots))
+        )
+    ]
+    for load in loads:
+        load.start()
     lat = lax.axis_index("lat")
     lon = lax.axis_index("lon")
     me = lat * N_LON + lon
@@ -167,6 +175,8 @@
         gone = src.at[pl.ds(0, NDEV - 1)]
         pltpu.make_async_copy(gone, gone, a2a_send.at[k]).wait()
 
+    for load in loads:
+        load.wait()
     for r in range(LAT):
         wown[r, :LEV, :] = zonal[:, r, :]
         wown[r, LEV:, :] = merid[:, r, :]
@@ -294,7 +304,7 @@
             proj[r, window * TYPES : (window + 1) * TYPES, :] = out[:8] + out[8:]
             return carry
 
-        lax.fori_loop(0, LAT, body, 0, unroll=4)
+        lax.fori_loop(0, LAT, body, 0, unroll=8)
 
     def message(dst, row):
         for w in range(WIN):
@@ -315,11 +325,11 @@
     def forward(it):
         ping, pong = field.at[0], field.at[1]
         project(0, lambda r: res[r + 4, :, :LON])
-        advance(pong, res, 4, 5, 19, False, 7)
-        advance(ping, pong, 0, 6, 18, False, 6)
+        advance(pong, res, 4, 5, 19, False, 14)
+        advance(ping, pong, 0, 6, 18, False, 12)
         project(1, lambda r: ping[r + 8, :, :LON])
-        advance(pong, ping, 0, 7, 17, False, 5)
-        advance(ping, pong, 0, 8, 16, False, 4)
+        advance(pong, ping, 0, 7, 17, False, 10)
+        advance(ping, pong, 0, 8, 16, False, 8)
         project(2, lambda r: ping[r + 8, :, :LON])
         for r in range(LAT):
             lgather[r * 48 : (r + 1) * 48, :] = jnp.concatenate(split(proj[r]), axis=0).astype(BF16)
@@ -394,44 +404,52 @@
             return c
 
         def outside(w):
+            count = near[w]
+            if count == 0:
+                return
+
             def body(i, c):
-                for k, g, r in ((0, 7 - i, 7 - i), (1, 16 + i, i)):
+                for k, g, r in ((0, i + 8 - count, i + 8 - count), (1, 16 + i, i)):
                     into[w][g, :, :LON] = forcing(ns_s[k, w * LAT + r])
                     into[w][g, :, LON:] = forcing(sside[g, w * TYPES : (w + 1) * TYPES, :])
                 return c
 
+            lax.fori_loop(0, count, body, 0, unroll=4 if count % 4 == 0 else count // 2)
+
+        def landed(w):
             if near[w]:
-                lax.fori_loop(0, near[w], body, 0, unroll=2)
-
-        lax.fori_loop(0, LAT, own, 0, unroll=2)
+                at = 6 + 2 * (2 - w)
+                for copy in copies[at : at + 2]:
+                    copy.wait()
+
+        lax.fori_loop(0, LAT, own, 0, unroll=4)
         for copy in copies[4:6]:
             copy.wait()
         for r, value in enumerate(sides(hp_s, 4)):
             sside[r + 8] = value
-        lax.fori_loop(0, LAT, own_side, 0, unroll=4)
-        advance(pong, ping, 0, 9, 15, True, 3)
+        lax.fori_loop(0, LAT, own_side, 0, unroll=8)
+        advance(pong, ping, 0, 9, 15, True, 6)
         for copy in copies[:4]:
             copy.wait()
         for r, value in enumerate(sides(hp_s, 0)):
             sside[r] = value
         for r, value in enumerate(sides(hp_s, 2)):
             sside[r + 16] = value
-        for copy in copies[6:]:
-            copy.wait()
-        for w in (2, 1, 0):
-            outside(w)
-        if deep:
-            advance(pong, ping, 0, 1, 9, True, 4)
-            advance(pong, ping, 0, 15, 23, True, 4)
-            advance(ping, pong, 0, 2, 22, True, 5, force1)
-            advance(pong, ping, 0, 3, 21, True, 6)
-            advance(ping, pong, 0, 4, 20, True, 4, force0)
-        else:
-            advance(pong, ping, 0, 5, 9, True, 4)
-            advance(pong, ping, 0, 15, 19, True, 4)
-            advance(ping, pong, 0, 6, 18, True, 6, force1)
-            advance(pong, ping, 0, 7, 17, True, 5)
-            advance(ping, pong, 0, 8, 16, True, 4, force0)
+        landed(2)
+        outside(2)
+        lo, hi = (1, 23) if deep else (5, 19)
+        advance(pong, ping, 0, lo, 9, True, 9 - lo)
+        advance(pong, ping, 0, 15, hi, True, hi - 15)
+        landed(1)
+        outside(1)
+        lo, hi = lo + 1, hi - 1
+        advance(ping, pong, 0, lo, hi, True, (hi - lo) // 2 if deep else hi - lo, force1)
+        lo, hi = lo + 1, hi - 1
+        advance(pong, ping, 0, lo, hi, True, (hi - lo) // 2 if deep else hi - lo)
+        landed(0)
+        outside(0)
+        lo, hi = lo + 1, hi - 1
+        advance(ping, pong, 0, lo, hi, True, 8, force0)
         zero = jnp.zeros((8, LON), F32)
 
         def done(acc):
@@ -566,6 +584,12 @@
     lax.fori_loop(0, 3, outer, 0)
 
 
+def flip(x_in, r_in, x_out, r_out):
+    for r in range(LAT):
+        x_out[:, r, :] = x_in[r]
+        r_out[:, r, :] = r_in[r]
+
+
 def shards(
     zonal_wind, merid_wind, operator_rows, innovation, error_weight, interp_weight, obs_slot,
     block_count, block_type, block_window, send_cols,
@@ -577,9 +601,14 @@
     x, r = pl.pallas_call(
         kernel,
         out_shape=[jax.ShapeDtypeStruct((LAT, CH, LON), F32)] * 2,
-        in_specs=[vm] * 10 + [sm] * 3,
+        in_specs=[pl.BlockSpec(memory_space=pl.ANY)] * 4 + [vm] * 6 + [sm] * 3,
         out_specs=[vm] * 2,
         scratch_shapes=[
+            V((LEV, LAT, LON), F32),
+            V((LEV, LAT, LON), F32),
+            V((KPTS, NBLK * ROWS), F32),
+            V((KPTS, NBLK * ROWS), jnp.int32),
+            dma((4,)),
             V((5, EXT, LEV, LANES), F32),
             V((2, EXT, CH, LANES), F32),
             V((MID, CH, LANES), F32),
@@ -630,13 +659,20 @@
         ),
         name="cg",
     )(
-        zonal_wind, merid_wind, operator_rows,
+        zonal_wind, merid_wind, interp_weight, obs_slot, operator_rows,
         innovation.reshape(NBLK, 1, ROWS), error_weight.reshape(NBLK, 1, ROWS),
-        interp_weight, obs_slot, send_cols, block_type.reshape(1, NBLK), block_window.reshape(1, NBLK),
+        send_cols, block_type.reshape(1, NBLK), block_window.reshape(1, NBLK),
         block_count, block_type, block_window,
     )
     shape = (4, LEV, LAT, LON)
-    return x.transpose(1, 0, 2).reshape(shape), r.transpose(1, 0, 2).reshape(shape)
+    x, r = pl.pallas_call(
+        flip,
+        out_shape=[jax.ShapeDtypeStruct((CH, LAT, LON), F32)] * 2,
+        in_specs=[vm] * 2,
+        out_specs=[vm] * 2,
+        name="flip",
+    )(x, r)
+    return x.reshape(shape), r.reshape(shape)
 
 
 def solution(mesh):

time: 107 us -> 99.3 us (0.928)
  Pallas kernels: 102 us -> 98.5 us
  local copies, waits for them, and re-layouts: 3.3 us -> 0 us
    pallas_call x1, Pallas kernels: 102 us -> 96 us  [shards(): pl.pallas_call(kernel, out_shape=[jax.ShapeDtypeStruct((LAT, CH, LON), F3...]
    unnamed x4 -> x0, local copies, waits for them, and re-layouts: 3.3 us -> none
    pallas_call x0 -> x1, Pallas kernels: none -> 2.49 us  [shards(): pl.pallas_call(flip, out_shape=[jax.ShapeDtypeStruct((CH, LAT, LON), F32)...]
where the time goes in v4:
time: 99.3 us; the launch traced here: 99.1 us
  Pallas kernels  98.5 us (99%)
    pallas_call x1, Pallas kernels, shards(): pl.pallas_call(kernel, out_shape=[jax.ShapeDtypeStruct((LAT, CH, LON), F3...  96 us
    pallas_call x1, Pallas kernels, shards(): pl.pallas_call(flip, out_shape=[jax.ShapeDtypeStruct((CH, LAT, LON), F32)...  2.49 us

profile of v4, /device:TPU:1, one launch (start us, length us, event | category | flops | bytes accessed | tf_op | source)
XLA Modules:
  0.0 99.1 jit_solution(14579684951650896555)
XLA Ops:
  0.6 96.0 %cg.1 = (f32[8,64,256]{2,1,0:T(8,128)}, f32[8,64,256]{2,1,0:T(8,128)}) custom-call(f32[16,8,256]{2,1,0:T(8,128)} %zonal_h.1, f32[16,8,256]{2,1,0:T(8,128)} %merid_h.1, f32[4,4096]{1,0:T(4,128)} %interp_h.1, s32[4,4096]{1,0:T(4,128)} %slots_h.1, f32[8,64]{1,0:T(8,128)} %rows_in.1, f32[32,1,128]{2,1,0:T(1,128)} %bitcast.6, f32[32,1,128]{2,1,0:T(1,128)} %bitcast.7, ...), custom_call_target="tpu_custom_call" | custom-call | tf_op jit(solution)/shard_map/cg/pallas_call | solution.py:601
  96.6 2.5 %flip.1 = (f32[64,8,256]{2,1,0:T(8,128)}, f32[64,8,256]{2,1,0:T(8,128)}) custom-call(f32[8,64,256]{2,1,0:T(8,128)} %get-tuple-element.6.x_in, f32[8,64,256]{2,1,0:T(8,128)} %get-tuple-element.7.r_in), custom_call_target="tpu_custom_call" | custom-call | tf_op jit(solution)/shard_map/flip/pallas_call | solution.py:668

commit v5 on v4

--- a/solution.py
+++ b/solution.py
@@ -36,6 +36,13 @@
     return high, value - high
 
 
+def exact(value):
+    high = value.astype(BF16)
+    rest = value - high.astype(F32)
+    middle = rest.astype(BF16)
+    return high, middle, (rest - middle.astype(F32)).astype(BF16)
+
+
 def mm(left, right):
     return jnp.dot(left, right, preferred_element_type=F32)
 
@@ -54,6 +61,37 @@
     return packed
 
 
+def pack_typed(rows):
+    packed = None
+    for r, row in enumerate(rows):
+        lane = lax.broadcasted_iota(jnp.int32, (row.shape[0], 128), 1)
+        even = pltpu.roll(row[:, :128], (4 + 16 * r) % 128, axis=1)
+        odd = pltpu.roll(row[:, 128:], (12 + 16 * r) % 128, axis=1)
+        moved = jnp.where((lane & 15) < 8, even, odd)
+        packed = moved if packed is None else jnp.where((lane >> 4) == r, moved, packed)
+    return packed
+
+
+def tiles(value):
+    return value[:, :128], value[:, 128:256], value[:, 256:]
+
+
+def west_of(parts):
+    even, odd, rim = parts
+    first = lax.broadcasted_iota(jnp.int32, even.shape, 1) == 0
+    odd = pltpu.roll(odd, 1, axis=1)
+    rim = pltpu.roll(rim, 1, axis=1)
+    return jnp.where(first, rim, odd), even, jnp.where(first, odd, rim)
+
+
+def east_of(parts):
+    even, odd, rim = parts
+    last = lax.broadcasted_iota(jnp.int32, even.shape, 1) == 127
+    even = pltpu.roll(even, 127, axis=1)
+    rim = pltpu.roll(rim, 127, axis=1)
+    return odd, jnp.where(last, rim, even), jnp.where(last, even, rim)
+
+
 def offsets():
     steps = [
         (dx, dc, dy, dz)
@@ -63,10 +101,11 @@
 
 
 def kernel(
-    zonal_h, merid_h, interp_h, slots_h, rows_in, innov, weight, cols, type_v, window_v,
-    count_s, type_s, window_s,
+    zonal_h, merid_h, interp_h, slots_h, rows_h, innov_h, weight_h, cols_h, typev_h, windowv_h,
+    count_h, type_h, window_h,
     x_out, r_out,
-    zonal, merid, interp, slots, in_sem, winds, field, res, dirn, inc, force0, force1, square, colq,
+    zonal, merid, interp, slots, rows_in, innov, weight, cols, type_v, window_v,
+    count_s, type_s, window_s, in_sem, winds, field, res, dirn, inc, force0, force1, square, colq, perm, mend, wnat,
     onehot, cweight, live, zrow, yrow, rblk, tsplit,
     colhot, proj, ssum, sside, stage, lgather, lscatter, sacc,
     send_f, send_b, recv_f, recv_b, wown,
@@ -76,7 +115,12 @@
     loads = [
         pltpu.make_async_copy(src, dst, in_sem.at[i])
         for i, (src, dst) in enumerate(
-            ((zonal_h, zonal), (merid_h, merid), (interp_h, interp), (slots_h, slots))
+            (
+                (slots_h, slots), (interp_h, interp), (count_h, count_s), (type_h, type_s),
+                (window_h, window_s), (weight_h, weight), (innov_h, innov), (cols_h, cols),
+                (rows_h, rows_in), (typev_h, type_v), (windowv_h, window_v), (zonal_h, zonal),
+                (merid_h, merid),
+            )
         )
     ]
     for load in loads:
@@ -163,24 +207,36 @@
     def a2a_start(src, dst, k, row_of, mine):
         def go(a, o):
             to(
-                src.at[row_of(a, o)], dst.at[mine], a, o, a2a_send.at[k], a2a_recv.at[k]
+                src.at[pl.ds(row_of(a, o) * 4, 4)], dst.at[pl.ds(mine * 4, 4)], a, o,
+                a2a_send.at[k], a2a_recv.at[k],
             ).start()
 
         everyone(go)
-        dst[mine] = src[row_of(lat, lon)]
+        dst[pl.ds(mine * 4, 4), :] = src[pl.ds(row_of(lat, lon) * 4, 4), :]
 
     def a2a_wait(src, dst, k):
-        got = dst.at[pl.ds(0, NDEV - 1)]
+        got = dst.at[pl.ds(0, 4 * (NDEV - 1))]
         pltpu.make_async_copy(got, got, a2a_recv.at[k]).wait()
-        gone = src.at[pl.ds(0, NDEV - 1)]
+        gone = src.at[pl.ds(0, 4 * (NDEV - 1))]
         pltpu.make_async_copy(gone, gone, a2a_send.at[k]).wait()
 
     for load in loads:
         load.wait()
     for r in range(LAT):
-        wown[r, :LEV, :] = zonal[:, r, :]
-        wown[r, LEV:, :] = merid[:, r, :]
-    pack_w[...] = pack_rows([wown[r] for r in range(LAT)])
+        wnat[r, :LEV, :] = zonal[:, r, :]
+        wnat[r, LEV:, :] = merid[:, r, :]
+    pack_w[...] = pack_rows([wnat[r] for r in range(LAT)])
+    natural = lax.broadcasted_iota(jnp.int32, (LON, LON), 0)
+    held = lax.broadcasted_iota(jnp.int32, (LON, LON), 1)
+    perm[...] = jnp.where(held == (natural & 1) * 128 + (natural >> 1), 1.0, 0.0).astype(BF16)
+    here = lax.broadcasted_iota(jnp.int32, (128, 128), 0)
+    there = lax.broadcasted_iota(jnp.int32, (128, 128), 1)
+    goal = (here & 112) + ((here >> 2) & 1) * 8 + 2 * (here & 3) + ((here >> 3) & 1)
+    mend[...] = jnp.where(there == goal, 1.0, 0.0).astype(BF16)
+    for i in range(4):
+        high, middle, low = exact(wnat[2 * i : 2 * i + 2].reshape(4 * LEV, LON))
+        value = mm(high, perm[...]) + mm(middle, perm[...]) + mm(low, perm[...])
+        wown[2 * i : 2 * i + 2] = value.reshape(2, 2 * LEV, LON)
 
     def tables(b, carry):
         at = pl.ds(pl.multiple_of(b * ROWS, ROWS), ROWS)
@@ -215,7 +271,7 @@
         return jnp.concatenate([colq[2 * n : 2 * n + 1, :], colq[2 * n + 1 : 2 * n + 2, :]], axis=1)
 
     for n in range(8):
-        low = columns(n) & 255
+        low = (columns(n) & 1) * 128 + ((columns(n) & 255) >> 1)
         sub = lax.broadcasted_iota(jnp.int32, (LON, 256), 0)
         colhot[n] = jnp.where(sub == low, 1.0, 0.0).astype(BF16)
     lane32 = lax.broadcasted_iota(jnp.int32, (CH, 32), 1)
@@ -238,10 +294,6 @@
     lax.fori_loop(0, LAT, clear, 0)
     rrv[...] = jnp.ones((1, 128), F32)
     part[...] = jnp.zeros((1, 128), F32)
-
-    pl.semaphore_wait(barrier, NDEV - 1)
-    for copy in halo_w():
-        copy.start()
 
     def build_winds():
         for copy in halo_w():
@@ -272,26 +324,26 @@
         def body(g, carry):
             for var in range(4):
                 at = slice(var * LEV, (var + 1) * LEV)
-                mid = src[g - shift, at, :]
-                below = src[g - shift - 1, at, :]
-                above = src[g - shift + 1, at, :]
+                mid = tiles(src[g - shift, at, :])
+                below = tiles(src[g - shift - 1, at, :])
+                above = tiles(src[g - shift + 1, at, :])
+                keep, from_west, from_east = (tiles(winds[i, g]) for i in range(3))
                 if adjoint:
-                    out = (
-                        winds[0, g] * mid
-                        + pltpu.roll(winds[1, g] * mid, LANES - 1, axis=1)
-                        + pltpu.roll(winds[2, g] * mid, 1, axis=1)
-                        + winds[3, g + 1] * above
-                        + winds[4, g - 1] * below
-                    )
+                    left = east_of([w * m for w, m in zip(from_west, mid)])
+                    right = west_of([w * m for w, m in zip(from_east, mid)])
+                    up, down = tiles(winds[3, g + 1]), tiles(winds[4, g - 1])
+                    up = [w * m for w, m in zip(up, above)]
+                    down = [w * m for w, m in zip(down, below)]
                 else:
-                    out = (
-                        winds[0, g] * mid
-                        + winds[1, g] * pltpu.roll(mid, 1, axis=1)
-                        + winds[2, g] * pltpu.roll(mid, LANES - 1, axis=1)
-                        + winds[3, g] * below
-                        + winds[4, g] * above
-                    )
-                dst[g, at, :] = out if extra is None else out + extra[g, at, :]
+                    left = [w * m for w, m in zip(from_west, west_of(mid))]
+                    right = [w * m for w, m in zip(from_east, east_of(mid))]
+                    up, down = tiles(winds[3, g]), tiles(winds[4, g])
+                    up = [w * m for w, m in zip(up, below)]
+                    down = [w * m for w, m in zip(down, above)]
+                for i in range(3):
+                    lanes = slice(i * 128, (i + 1) * 128)
+                    out = keep[i] * mid[i] + left[i] + right[i] + up[i] + down[i]
+                    dst[g, at, lanes] = out if extra is None else out + extra[g, at, lanes]
             return carry
 
         lax.fori_loop(lo, hi, body, 0, unroll=unroll)
@@ -308,11 +360,11 @@
 
     def message(dst, row):
         for w in range(WIN):
-            dst[:, w, :] = stage[w * 128 : (w + 1) * 128, :].T
-        dst[:, 3, :] = jnp.broadcast_to(row, (NDEV, 128))
+            dst[pl.ds(w, NDEV, stride=4), :] = stage[w * 128 : (w + 1) * 128, :].T
+        dst[pl.ds(3, NDEV, stride=4), :] = jnp.broadcast_to(row, (NDEV, 128))
 
     def total(recv):
-        lanes = jnp.sum(recv[:, 3, :], axis=0, keepdims=True)
+        lanes = jnp.sum(recv[pl.ds(3, NDEV, stride=4), :], axis=0, keepdims=True)
         return jnp.broadcast_to(jnp.sum(lanes, axis=1, keepdims=True), (1, 128))
 
     def full(row):
@@ -352,7 +404,7 @@
         beta = jnp.where(it == 1, jnp.zeros_like(norm), norm / rrv[...])
         rrv[...] = norm
         for w in range(WIN):
-            table = recv_f[:, w, :].T
+            table = recv_f[pl.ds(w, NDEV, stride=4), :].T
             high, low = split(table)
             for t in range(TYPES):
                 at = slice(t * 16, (t + 1) * 16)
@@ -497,37 +549,49 @@
 
             def body(r, c):
                 p = dirn[r + 4, :, :LON]
-                x_out[r] = inc[r] + narrow * p
-                r_out[r] = res[r + 4, :, :LON] - narrow * (p + ping[r + 8, :, :LON])
+                value = jnp.concatenate(
+                    [
+                        inc[r] + narrow * p,
+                        res[r + 4, :, :LON] - narrow * (p + ping[r + 8, :, :LON]),
+                    ],
+                    axis=0,
+                )
+                high, middle, low = exact(value)
+                value = mm_nt(high, perm[...]) + mm_nt(middle, perm[...]) + mm_nt(low, perm[...])
+                x_out[r] = value[:CH]
+                r_out[r] = value[CH:]
                 return c
 
             lax.fori_loop(0, LAT, body, 0, unroll=2)
 
-    def outer(it, carry):
-        @pl.when(it > 0)
-        def _():
-            forward(it)
-
+    def observe():
         def spread(b, c):
             z = zrow[b]
             value = cweight[b] * jnp.concatenate([z, z, z, z], axis=1)
             high, low = split(value)
             both = jnp.concatenate([high, low], axis=0).astype(BF16)
             out = mm_nt(both, onehot[b])
-            rblk[b] = out[:16] + out[16:]
+            rblk[pl.ds(pl.multiple_of(b * SLOTS, SLOTS), SLOTS), :] = out[:16] + out[16:]
             return c
 
         lax.fori_loop(0, NBLK, spread, 0, unroll=8)
         for q in range(SLOTS):
-            high, low = split(rblk[:, q, :])
+            high, low = split(rblk[pl.ds(q, NBLK, stride=SLOTS), :])
             out = mm(member, high.astype(BF16)) + mm(member, low.astype(BF16))
             for w in range(WIN):
                 stage[pl.ds(w * 128 + q, 8, stride=16), :] = out[w * 8 : (w + 1) * 8]
         message(send_b, part[...])
+
+    observe()
+    pl.semaphore_wait(barrier, NDEV - 1)
+
+    def outer(it, carry):
         a2a_start(send_b, recv_b, 1, plain, swapped(lat, lon))
 
         @pl.when(it == 0)
         def _():
+            for copy in halo_w():
+                copy.start()
             build_winds()
 
         @pl.when(it == 1)
@@ -541,7 +605,7 @@
 
         a2a_wait(send_b, recv_b, 1)
         for w in range(WIN):
-            stage[w * 128 : (w + 1) * 128, :] = recv_b[:, w, :].T
+            stage[w * 128 : (w + 1) * 128, :] = recv_b[pl.ds(w, NDEV, stride=4), :].T
         alpha = rrv[...] / total(recv_b)
         for n in range(8):
             halves = []
@@ -568,12 +632,16 @@
             value = sacc[r * 48 : r * 48 + WT, :] + sacc[r * 48 + WT : (r + 1) * 48, :]
             for w in range(WIN):
                 ssum[w * LAT + r] = value[w * TYPES : (w + 1) * TYPES]
-        pack_s[...] = pack_rows(
+        mixed = pack_typed(
             [jnp.concatenate([ssum[w * LAT + r] for w in range(WIN)], axis=0) for r in range(LAT)]
         )
+        mixed = mm(jnp.concatenate(split(mixed), axis=0).astype(BF16), mend[...])
+        pack_s[...] = mixed[:WT] + mixed[WT:]
         @pl.when(it < 2)
         def _():
             adjoint(it, alpha, True)
+            forward(it + 1)
+            observe()
 
         @pl.when(it == 2)
         def _():
@@ -595,20 +663,28 @@
     block_count, block_type, block_window, send_cols,
 ):
     vm = pl.BlockSpec(memory_space=pltpu.VMEM)
-    sm = pl.BlockSpec(memory_space=pltpu.SMEM)
     V = pltpu.VMEM
     dma = pltpu.SemaphoreType.DMA
     x, r = pl.pallas_call(
         kernel,
         out_shape=[jax.ShapeDtypeStruct((LAT, CH, LON), F32)] * 2,
-        in_specs=[pl.BlockSpec(memory_space=pl.ANY)] * 4 + [vm] * 6 + [sm] * 3,
+        in_specs=[pl.BlockSpec(memory_space=pl.ANY)] * 13,
         out_specs=[vm] * 2,
         scratch_shapes=[
             V((LEV, LAT, LON), F32),
             V((LEV, LAT, LON), F32),
             V((KPTS, NBLK * ROWS), F32),
             V((KPTS, NBLK * ROWS), jnp.int32),
-            dma((4,)),
+            V((TYPES, CH), F32),
+            V((NBLK, 1, ROWS), F32),
+            V((NBLK, 1, ROWS), F32),
+            V((1, NDEV * SLOTS), jnp.int32),
+            V((1, NBLK), jnp.int32),
+            V((1, NBLK), jnp.int32),
+            pltpu.SMEM((NBLK,), jnp.int32),
+            pltpu.SMEM((NBLK,), jnp.int32),
+            pltpu.SMEM((NBLK,), jnp.int32),
+            dma((13,)),
             V((5, EXT, LEV, LANES), F32),
             V((2, EXT, CH, LANES), F32),
             V((MID, CH, LANES), F32),
@@ -618,12 +694,15 @@
             V((EXT, CH, LANES), F32),
             V((128, 128), F32),
             V((SLOTS, 128), jnp.int32),
+            V((LON, LON), BF16),
+            V((128, 128), BF16),
+            V((LAT, 2 * LEV, LON), F32),
             V((NBLK, NDEV, KPTS * ROWS), BF16),
             V((NBLK, SLOTS, KPTS * ROWS), F32),
             V((NBLK, 1, ROWS), F32),
             V((NBLK, 1, ROWS), F32),
             V((NBLK, 1, ROWS), F32),
-            V((NBLK, SLOTS, NDEV), F32),
+            V((NBLK * SLOTS, NDEV), F32),
             V((WT, 32, NDEV), BF16),
             V((8, LON, 256), BF16),
             V((LAT, WT, LON), F32),
@@ -633,10 +712,10 @@
             V((16 * WT, 256), BF16),
             V((16 * WT, 256), BF16),
             V((16 * WT, 256), F32),
-            V((NDEV, 4, 128), F32),
-            V((NDEV, 4, 128), F32),
-            V((NDEV, 4, 128), F32),
-            V((NDEV, 4, 128), F32),
+            V((NDEV * 4, 128), F32),
+            V((NDEV * 4, 128), F32),
+            V((NDEV * 4, 128), F32),
+            V((NDEV * 4, 128), F32),
             V((LAT, 2 * LEV, LON), F32),
             V((2 * LEV, 128), F32),
             V((WT, 128), F32),

time: 99.3 us -> 96.7 us (0.974)
  Pallas kernels: 98.5 us -> 95.9 us
    pallas_call x1, Pallas kernels: 96 us -> 93.4 us  [shards(): pl.pallas_call(kernel, out_shape=[jax.ShapeDtypeStruct((LAT, CH, LON), F3...]
where the time goes in v5:
time: 96.7 us; the launch traced here: 96.6 us
  Pallas kernels  95.9 us (99%)
    pallas_call x1, Pallas kernels, shards(): pl.pallas_call(kernel, out_shape=[jax.ShapeDtypeStruct((LAT, CH, LON), F3...  93.4 us
    pallas_call x1, Pallas kernels, shards(): pl.pallas_call(flip, out_shape=[jax.ShapeDtypeStruct((CH, LAT, LON), F32)...  2.49 us

profile of v5, /device:TPU:1, one launch (start us, length us, event | category | flops | bytes accessed | tf_op | source)
XLA Modules:
  0.0 96.6 jit_solution(3355646400110983770)
XLA Ops:
  0.6 93.4 %cg.1 = (f32[8,64,256]{2,1,0:T(8,128)}, f32[8,64,256]{2,1,0:T(8,128)}) custom-call(f32[16,8,256]{2,1,0:T(8,128)} %zonal_h.1, f32[16,8,256]{2,1,0:T(8,128)} %merid_h.1, f32[4,4096]{1,0:T(4,128)} %interp_h.1, s32[4,4096]{1,0:T(4,128)} %slots_h.1, f32[8,64]{1,0:T(8,128)} %rows_h.1, f32[32,1,128]{2,1,0:T(1,128)} %bitcast.6, f32[32,1,128]{2,1,0:T(1,128)} %bitcast.7, ...), custom_call_target="tpu_custom_call" | custom-call | tf_op jit(solution)/shard_map/cg/pallas_call | solution.py:668
  94.1 2.5 %flip.1 = (f32[64,8,256]{2,1,0:T(8,128)}, f32[64,8,256]{2,1,0:T(8,128)}) custom-call(f32[8,64,256]{2,1,0:T(8,128)} %get-tuple-element.6.x_in, f32[8,64,256]{2,1,0:T(8,128)} %get-tuple-element.7.r_in), custom_call_target="tpu_custom_call" | custom-call | tf_op jit(solution)/shard_map/flip/pallas_call | solution.py:747

commit v6 on v5

--- a/solution.py
+++ b/solution.py
@@ -109,7 +109,7 @@
     onehot, cweight, live, zrow, yrow, rblk, tsplit,
     colhot, proj, ssum, sside, stage, lgather, lscatter, sacc,
     send_f, send_b, recv_f, recv_b, wown,
-    pack_w, pack_s, ns_w, ns_s, hp_w, hp_s, rrv, part, betav,
+    pack_w, pack_s, ns_w, ns_s, hp_w, hp_s, rrv, part, rpart, betav, back, x_held, r_held, out_sem,
     a2a_send, a2a_recv, hw_send, hw_recv, hs_send, hs_recv,
 ):
     loads = [
@@ -204,20 +204,20 @@
         both = jnp.where((lane & 15) < 8, hp[base], hp[base + 1])
         return [pltpu.roll(both, (256 - 16 * r - 8) % 128, axis=1) for r in range(LAT)]
 
-    def a2a_start(src, dst, k, row_of, mine):
+    def a2a_start(src, dst, k, row_of, mine, rows):
         def go(a, o):
             to(
-                src.at[pl.ds(row_of(a, o) * 4, 4)], dst.at[pl.ds(mine * 4, 4)], a, o,
+                src.at[pl.ds(row_of(a, o) * 4, rows)], dst.at[pl.ds(mine * 4, rows)], a, o,
                 a2a_send.at[k], a2a_recv.at[k],
             ).start()
 
         everyone(go)
         dst[pl.ds(mine * 4, 4), :] = src[pl.ds(row_of(lat, lon) * 4, 4), :]
 
-    def a2a_wait(src, dst, k):
-        got = dst.at[pl.ds(0, 4 * (NDEV - 1))]
+    def a2a_wait(src, dst, k, rows):
+        got = dst.at[pl.ds(0, rows * (NDEV - 1))]
         pltpu.make_async_copy(got, got, a2a_recv.at[k]).wait()
-        gone = src.at[pl.ds(0, 4 * (NDEV - 1))]
+        gone = src.at[pl.ds(0, rows * (NDEV - 1))]
         pltpu.make_async_copy(gone, gone, a2a_send.at[k]).wait()
 
     for load in loads:
@@ -229,6 +229,7 @@
     natural = lax.broadcasted_iota(jnp.int32, (LON, LON), 0)
     held = lax.broadcasted_iota(jnp.int32, (LON, LON), 1)
     perm[...] = jnp.where(held == (natural & 1) * 128 + (natural >> 1), 1.0, 0.0).astype(BF16)
+    back[...] = jnp.where(held == (natural & 127) * 2 + (natural >> 7), 1.0, 0.0).astype(BF16)
     here = lax.broadcasted_iota(jnp.int32, (128, 128), 0)
     there = lax.broadcasted_iota(jnp.int32, (128, 128), 1)
     goal = (here & 112) + ((here >> 2) & 1) * 8 + 2 * (here & 3) + ((here >> 3) & 1)
@@ -293,6 +294,7 @@
 
     lax.fori_loop(0, LAT, clear, 0)
     rrv[...] = jnp.ones((1, 128), F32)
+    rpart[...] = jnp.zeros((1, 128), F32)
     part[...] = jnp.zeros((1, 128), F32)
 
     def build_winds():
@@ -363,9 +365,16 @@
             dst[pl.ds(w, NDEV, stride=4), :] = stage[w * 128 : (w + 1) * 128, :].T
         dst[pl.ds(3, NDEV, stride=4), :] = jnp.broadcast_to(row, (NDEV, 128))
 
-    def total(recv):
-        lanes = jnp.sum(recv[pl.ds(3, NDEV, stride=4), :], axis=0, keepdims=True)
+    def received(recv):
+        return jnp.sum(recv[pl.ds(3, NDEV, stride=4), :], axis=0, keepdims=True)
+
+    def spread_sum(lanes):
         return jnp.broadcast_to(jnp.sum(lanes, axis=1, keepdims=True), (1, 128))
+
+    lower = lax.broadcasted_iota(jnp.int32, (1, 128), 1) < 64
+
+    def fold(row):
+        return row + pltpu.roll(row, 64, axis=1)
 
     def full(row):
         return jnp.concatenate([row, row, row], axis=1)
@@ -397,12 +406,22 @@
                     stage[pl.ds(w * 128 + 2 * n + half, 8, stride=16), :] = got[
                         w * 8 : (w + 1) * 8, half * 128 : (half + 1) * 128
                     ]
-        message(send_f, part[...])
-        a2a_start(send_f, recv_f, 0, swapped, me)
-        a2a_wait(send_f, recv_f, 0)
-        norm = total(recv_f)
+        message(send_f, rpart[...])
+
+        def exchange(rows):
+            a2a_start(send_f, recv_f, 0, swapped, me, rows)
+            a2a_wait(send_f, recv_f, 0, rows)
+
+        @pl.when(it == 1)
+        def _():
+            exchange(3)
+
+        @pl.when(it > 1)
+        def _():
+            exchange(4)
+
+        norm = spread_sum(received(recv_f))
         beta = jnp.where(it == 1, jnp.zeros_like(norm), norm / rrv[...])
-        rrv[...] = norm
         for w in range(WIN):
             table = recv_f[pl.ds(w, NDEV, stride=4), :].T
             high, low = split(table)
@@ -433,6 +452,20 @@
         part[...] = quad + pp[:, :128] + pp[:, 128:]
         betav[...] = beta
 
+    def row_copy(i):
+        held_rows, out = (x_held, x_out) if i < LAT else (r_held, r_out)
+        return pltpu.make_async_copy(held_rows.at[i % LAT], out.at[:, i % LAT, :], out_sem.at[i])
+
+    left = inc
+
+    def restore(dst, out, base, group, row):
+        rows = range(4 * group, 4 * group + 4)
+        high, middle, low = exact(jnp.concatenate([row(r) for r in rows], axis=0))
+        value = mm(high, back[...]) + mm(middle, back[...]) + mm(low, back[...])
+        for i, r in enumerate(rows):
+            dst[r] = value[i * CH : (i + 1) * CH]
+            row_copy(base + r).start()
+
     def forcing(value):
         high, low = split(value)
         return mm(opt, jnp.concatenate([high, high, low, low], axis=0).astype(BF16))
@@ -474,6 +507,12 @@
                 for copy in copies[at : at + 2]:
                     copy.wait()
 
+        if not deep:
+            narrow = full(alpha)[:, :LON]
+            for group in range(2):
+                restore(x_held, x_out, 0, group, lambda r: inc[r] + narrow * dirn[r + 4, :, :LON])
+            for r in range(LAT):
+                left[r] = res[r + 4, :, :LON] - narrow * dirn[r + 4, :, :LON]
         lax.fori_loop(0, LAT, own, 0, unroll=4)
         for copy in copies[4:6]:
             copy.wait()
@@ -506,7 +545,7 @@
 
         def done(acc):
             acc = jnp.sum(acc, axis=0, keepdims=True)
-            part[...] = acc[:, :128] + acc[:, 128:]
+            rpart[...] = acc[:, :128] + acc[:, 128:]
 
         scale = full(alpha)
         if deep:
@@ -545,24 +584,13 @@
                 lax.fori_loop(0, 8, rim, 0)
                 done(lax.fori_loop(0, LAT, body, zero, unroll=2))
         else:
-            narrow = scale[:, :LON]
-
-            def body(r, c):
-                p = dirn[r + 4, :, :LON]
-                value = jnp.concatenate(
-                    [
-                        inc[r] + narrow * p,
-                        res[r + 4, :, :LON] - narrow * (p + ping[r + 8, :, :LON]),
-                    ],
-                    axis=0,
+            for group in range(2):
+                restore(
+                    r_held, r_out, LAT, group,
+                    lambda r: left[r] - scale[:, :LON] * ping[r + 8, :, :LON],
                 )
-                high, middle, low = exact(value)
-                value = mm_nt(high, perm[...]) + mm_nt(middle, perm[...]) + mm_nt(low, perm[...])
-                x_out[r] = value[:CH]
-                r_out[r] = value[CH:]
-                return c
-
-            lax.fori_loop(0, LAT, body, 0, unroll=2)
+            for i in range(2 * LAT):
+                row_copy(i).wait()
 
     def observe():
         def spread(b, c):
@@ -580,13 +608,20 @@
             out = mm(member, high.astype(BF16)) + mm(member, low.astype(BF16))
             for w in range(WIN):
                 stage[pl.ds(w * 128 + q, 8, stride=16), :] = out[w * 8 : (w + 1) * 8]
-        message(send_b, part[...])
+        message(send_b, jnp.where(lower, fold(part[...]), fold(rpart[...])))
 
     observe()
     pl.semaphore_wait(barrier, NDEV - 1)
 
     def outer(it, carry):
-        a2a_start(send_b, recv_b, 1, plain, swapped(lat, lon))
+        @pl.when(it == 0)
+        def _():
+            a2a_start(send_b, recv_b, 1, plain, swapped(lat, lon), 3)
+
+        @pl.when(it > 0)
+        def _():
+            a2a_start(send_b, recv_b, 1, plain, swapped(lat, lon), 4)
+
 
         @pl.when(it == 0)
         def _():
@@ -603,10 +638,20 @@
 
             lax.fori_loop(0, 8, beyond, 0)
 
-        a2a_wait(send_b, recv_b, 1)
+        @pl.when(it == 0)
+        def _():
+            a2a_wait(send_b, recv_b, 1, 3)
+
+        @pl.when(it > 0)
+        def _():
+            a2a_wait(send_b, recv_b, 1, 4)
+
         for w in range(WIN):
             stage[w * 128 : (w + 1) * 128, :] = recv_b[pl.ds(w, NDEV, stride=4), :].T
-        alpha = rrv[...] / total(recv_b)
+        sums = received(recv_b)
+        norm = spread_sum(jnp.where(lower, 0.0, sums))
+        rrv[...] = norm
+        alpha = norm / spread_sum(jnp.where(lower, sums, 0.0))
         for n in range(8):
             halves = []
             for half in range(2):
@@ -652,24 +697,33 @@
     lax.fori_loop(0, 3, outer, 0)
 
 
-def flip(x_in, r_in, x_out, r_out):
-    for r in range(LAT):
-        x_out[:, r, :] = x_in[r]
-        r_out[:, r, :] = r_in[r]
+def relay(x_in, r_in, x_out, r_out, held, load, store):
+    loads, stores = [], []
+    for i in range(8):
+        src, dst = (x_in, x_out) if i < 4 else (r_in, r_out)
+        at = pl.ds(i % 4 * LEV, LEV)
+        loads.append(pltpu.make_async_copy(src.at[at], held.at[i], load.at[i]))
+        stores.append(pltpu.make_async_copy(held.at[i], dst.at[at], store.at[i]))
+    for copy in loads:
+        copy.start()
+    for first, second in zip(loads, stores):
+        first.wait()
+        second.start()
+    for copy in stores:
+        copy.wait()
 
 
 def shards(
     zonal_wind, merid_wind, operator_rows, innovation, error_weight, interp_weight, obs_slot,
     block_count, block_type, block_window, send_cols,
 ):
-    vm = pl.BlockSpec(memory_space=pltpu.VMEM)
     V = pltpu.VMEM
     dma = pltpu.SemaphoreType.DMA
     x, r = pl.pallas_call(
         kernel,
-        out_shape=[jax.ShapeDtypeStruct((LAT, CH, LON), F32)] * 2,
+        out_shape=[jax.ShapeDtypeStruct((CH, LAT, LON), F32)] * 2,
         in_specs=[pl.BlockSpec(memory_space=pl.ANY)] * 13,
-        out_specs=[vm] * 2,
+        out_specs=[pl.BlockSpec(memory_space=pl.ANY)] * 2,
         scratch_shapes=[
             V((LEV, LAT, LON), F32),
             V((LEV, LAT, LON), F32),
@@ -726,6 +780,11 @@
             V((1, 128), F32),
             V((1, 128), F32),
             V((1, 128), F32),
+            V((1, 128), F32),
+            V((LON, LON), BF16),
+            V((LAT, CH, LON), F32),
+            V((LAT, CH, LON), F32),
+            dma((2 * LAT,)),
             dma((2,)),
             dma((2,)),
             dma((8,)),
@@ -744,12 +803,19 @@
         block_count, block_type, block_window,
     )
     shape = (4, LEV, LAT, LON)
+    hbm = pl.BlockSpec(memory_space=pl.ANY)
     x, r = pl.pallas_call(
-        flip,
+        relay,
         out_shape=[jax.ShapeDtypeStruct((CH, LAT, LON), F32)] * 2,
-        in_specs=[vm] * 2,
-        out_specs=[vm] * 2,
-        name="flip",
+        in_specs=[hbm] * 2,
+        out_specs=[hbm] * 2,
+        scratch_shapes=[
+            pltpu.VMEM((8, LEV, LAT, LON), F32),
+            pltpu.SemaphoreType.DMA((8,)),
+            pltpu.SemaphoreType.DMA((8,)),
+        ],
+        compiler_params=pltpu.CompilerParams(vmem_limit_bytes=60 << 20),
+        name="relay",
     )(x, r)
     return x.reshape(shape), r.reshape(shape)
 

time: 96.7 us -> 94.3 us (0.975)
  Pallas kernels: 95.9 us -> 93.5 us
    pallas_call x2, Pallas kernels: 95.9 us -> 93.5 us  [the longest x1 91.4 us: shards(): pl.pallas_call(kernel, out_shape=[jax.ShapeDtypeStruct((CH, LAT, LON), F3...]
where the time goes in v6:
time: 94.3 us; the launch traced here: 94.2 us
  Pallas kernels  93.5 us (99%)
    pallas_call x1, Pallas kernels, shards(): pl.pallas_call(kernel, out_shape=[jax.ShapeDtypeStruct((CH, LAT, LON), F3...  91.4 us
    pallas_call x1, Pallas kernels, shards(): pl.pallas_call(relay, out_shape=[jax.ShapeDtypeStruct((CH, LAT, LON), F32...  2.09 us

profile of v6, /device:TPU:1, one launch (start us, length us, event | category | flops | bytes accessed | tf_op | source)
XLA Modules:
  0.0 94.2 jit_solution(14448645051524082277)
XLA Ops:
  0.6 91.4 %cg.1 = (f32[64,8,256]{2,1,0:T(8,128)}, f32[64,8,256]{2,1,0:T(8,128)}) custom-call(f32[16,8,256]{2,1,0:T(8,128)} %zonal_h.1, f32[16,8,256]{2,1,0:T(8,128)} %merid_h.1, f32[4,4096]{1,0:T(4,128)} %interp_h.1, s32[4,4096]{1,0:T(4,128)} %slots_h.1, f32[8,64]{1,0:T(8,128)} %rows_h.1, f32[32,1,128]{2,1,0:T(1,128)} %bitcast.6, f32[32,1,128]{2,1,0:T(1,128)} %bitcast.7, ...), custom_call_target="tpu_custom_call" | custom-call | tf_op jit(solution)/shard_map/cg/pallas_call | solution.py:722
  92.1 2.1 %relay.1 = (f32[64,8,256]{2,1,0:T(8,128)}, f32[64,8,256]{2,1,0:T(8,128)}) custom-call(f32[64,8,256]{2,1,0:T(8,128)} %get-tuple-element.6.x_in, f32[64,8,256]{2,1,0:T(8,128)} %get-tuple-element.7.r_in), custom_call_target="tpu_custom_call" | custom-call | tf_op jit(solution)/shard_map/relay/pallas_call | solution.py:807

commit v7 on v6

--- a/solution.py
+++ b/solution.py
@@ -258,7 +258,7 @@
         yrow[b] = jnp.zeros((1, ROWS), F32)
         return carry
 
-    lax.fori_loop(0, NBLK, tables, 0, unroll=2)
+    lax.fori_loop(0, NBLK, tables, 0, unroll=4)
     raw = jnp.concatenate([cols[:, a * 128 : (a + 1) * 128] for a in range(16)], axis=0).astype(F32)
     sub16 = lax.broadcasted_iota(jnp.int32, (16, 128), 0)
     lane16 = lax.broadcasted_iota(jnp.int32, (16, 128), 1) & 15
@@ -440,7 +440,7 @@
             zrow[b] = z
             return acc + z * y
 
-        quad = lax.fori_loop(0, NBLK, look, jnp.zeros((1, ROWS), F32), unroll=8)
+        quad = lax.fori_loop(0, NBLK, look, jnp.zeros((1, ROWS), F32), unroll=16)
 
         def turn(r, acc):
             p = res[r + 4] + full(beta) * dirn[r + 4]
@@ -536,7 +536,7 @@
         lo, hi = lo + 1, hi - 1
         advance(ping, pong, 0, lo, hi, True, (hi - lo) // 2 if deep else hi - lo, force1)
         lo, hi = lo + 1, hi - 1
-        advance(pong, ping, 0, lo, hi, True, (hi - lo) // 2 if deep else hi - lo)
+        advance(pong, ping, 0, lo, hi, True, hi - lo)
         landed(0)
         outside(0)
         lo, hi = lo + 1, hi - 1
@@ -602,7 +602,7 @@
             rblk[pl.ds(pl.multiple_of(b * SLOTS, SLOTS), SLOTS), :] = out[:16] + out[16:]
             return c
 
-        lax.fori_loop(0, NBLK, spread, 0, unroll=8)
+        lax.fori_loop(0, NBLK, spread, 0, unroll=16)
         for q in range(SLOTS):
             high, low = split(rblk[pl.ds(q, NBLK, stride=SLOTS), :])
             out = mm(member, high.astype(BF16)) + mm(member, low.astype(BF16))

time: 94.3 us -> 93.1 us (0.987)
  Pallas kernels: 93.5 us -> 92.1 us
    pallas_call x1, Pallas kernels: 91.4 us -> 90 us  [shards(): pl.pallas_call(kernel, out_shape=[jax.ShapeDtypeStruct((CH, LAT, LON), F3...]
where the time goes in v7:
time: 93.1 us; the launch traced here: 92.9 us
  Pallas kernels  92.1 us (99%)
    pallas_call x1, Pallas kernels, shards(): pl.pallas_call(kernel, out_shape=[jax.ShapeDtypeStruct((CH, LAT, LON), F3...  90 us
    pallas_call x1, Pallas kernels, shards(): pl.pallas_call(relay, out_shape=[jax.ShapeDtypeStruct((CH, LAT, LON), F32...  2.09 us

profile of v7, /device:TPU:1, one launch (start us, length us, event | category | flops | bytes accessed | tf_op | source)
XLA Modules:
  0.0 92.9 jit_solution(16618284622405287101)
XLA Ops:
  0.6 90.0 %cg.1 = (f32[64,8,256]{2,1,0:T(8,128)}, f32[64,8,256]{2,1,0:T(8,128)}) custom-call(f32[16,8,256]{2,1,0:T(8,128)} %zonal_h.1, f32[16,8,256]{2,1,0:T(8,128)} %merid_h.1, f32[4,4096]{1,0:T(4,128)} %interp_h.1, s32[4,4096]{1,0:T(4,128)} %slots_h.1, f32[8,64]{1,0:T(8,128)} %rows_h.1, f32[32,1,128]{2,1,0:T(1,128)} %bitcast.6, f32[32,1,128]{2,1,0:T(1,128)} %bitcast.7, ...), custom_call_target="tpu_custom_call" | custom-call | tf_op jit(solution)/shard_map/cg/pallas_call | solution.py:722
  90.6 2.1 %relay.1 = (f32[64,8,256]{2,1,0:T(8,128)}, f32[64,8,256]{2,1,0:T(8,128)}) custom-call(f32[64,8,256]{2,1,0:T(8,128)} %get-tuple-element.6.x_in, f32[64,8,256]{2,1,0:T(8,128)} %get-tuple-element.7.r_in), custom_call_target="tpu_custom_call" | custom-call | tf_op jit(solution)/shard_map/relay/pallas_call | solution.py:807
